TPU v7x, 256 devices: a whole 4x4x8 slice. The times are simulated.
256 devices in a mesh: box: 256 (over y, z, x, core).
Axes of the slice: x: 4, y: 4, z: 8, core: 2. Of those that a mesh axis runs over, the one named last changes fastest.
Arguments:
- basis_vector: float32 [16, 1048576], P(None, 'box'), may hold values from -600 to 600
- diagonal: float32 [1048576], P('box'), may hold values from 0.25 to 2
- coords: int32 [2, 1048576], P(None, 'box'), may hold values from 0 to 4095
- phase_scale: int32 [1], replicated, may hold values from 1 to 8190
- sketch_rows: int32 [1048576], P('box'), may hold values from 0 to 2047
- sketch_signs: int32 [1048576], P('box'), may hold values from 0 to 1
Outputs:
- new_basis: float32 [16, 1048576], P(None, 'box')
- sketch: float32 [16, 2048], replicated
- arnoldi: float32 [2, 16], replicated
All inputs are finite; a program needn't handle non-finite values.
Results may differ from a plain program's by a relative error of at most 0.00019.
Values sent between devices are 32-bit elements; how exact they have to be, the bound alone decides.
No kernel may reach another device: no remote copies, remote signals or barrier semaphores. Data moves between devices by JAX's collectives and lax.ppermute only.
A program may use at most 64 MiB of HBM per device.

v0:
```python
import functools
import math

import jax
import jax.numpy as jnp
from jax import lax
from jax.sharding import Mesh
from jax.sharding import PartitionSpec as P

RANK = 16
WIDTH = 32
LEAF = 32
SKETCH = 2048
BOX = ("box_0", "box_1", "box_2", "box_3")


modulus = 8191
epsilon = 1e-06


def swapped(x, axis, bit):
    return lax.ppermute(x, axis, [(i, i ^ 1 << bit) for i in range(lax.axis_size(axis))])


def one_axis_at_a_time(x, axes):
    return functools.reduce(lax.psum, axes, x)


def leaf_table(coords, phase_scale):
    scale_mod = phase_scale[0] % modulus
    freq = jnp.arange(RANK, dtype=jnp.int32)
    freq_first = freq % 4 + 1
    freq_second = freq // 4 + 1
    linear = (
        freq_first[:, None] * coords[0][None, :] + freq_second[:, None] * coords[1][None, :]
    ) % modulus
    phase = scale_mod * linear % modulus
    angle = phase.astype(jnp.float32) * (2.0 * math.pi / modulus)
    return jnp.concatenate([jnp.cos(angle), jnp.sin(angle)], 0) * (1.0 / math.sqrt(LEAF))


def translations(box_ids, segment_num, phase_scale):
    scale_mod = phase_scale[0] % modulus
    base_key = (box_ids * 37 + 101 * segment_num) % (modulus - 1) + 1
    unit_phase = scale_mod * base_key % modulus
    indices = jnp.arange(WIDTH, dtype=jnp.int32)
    prod_a = (indices[:, None] + 1) * (indices[None, :] + 2) % modulus
    prod_b = (indices[:, None] + 3) * (indices[None, :] + 1) % modulus
    phase_a = prod_a[:, :, None] * unit_phase[None, None, :] % modulus
    phase_b = (prod_b[:, :, None] * unit_phase[None, None, :] + 4096) % modulus
    factor = 2.0 * math.pi / modulus
    ident = jnp.eye(WIDTH, dtype=jnp.float32)[:, :, None]
    own_map = 0.85 * ident + 0.35 / math.sqrt(WIDTH) * jnp.cos(phase_a.astype(jnp.float32) * factor)
    cross_map = 0.6 / math.sqrt(WIDTH) * jnp.cos(phase_b.astype(jnp.float32) * factor)
    return (own_map, cross_map)


def mix(matrix, coeffs):
    return jnp.einsum("wvg,vgq->wgq", matrix, coeffs, precision=lax.Precision.HIGHEST)


def one_segment(coeffs, segment_num, group_boxes, phase_scale):
    own_map, cross_map = translations(group_boxes, segment_num, phase_scale)
    partner = swapped(coeffs, BOX, segment_num)
    return mix(own_map, coeffs) + mix(cross_map, partner)


def body(basis_vector, diagonal, coords, phase_scale, sketch_rows, sketch_signs):
    highest = lax.Precision.HIGHEST
    columns, local_points = basis_vector.shape
    box_count = local_points // LEAF
    devices = lax.axis_size(BOX)
    segment_count = devices.bit_length() - 1
    rank_id = lax.axis_index(BOX)
    local_ids = jnp.arange(box_count, dtype=jnp.int32)
    group_boxes = rank_id * box_count + local_ids
    leaf_map = leaf_table(coords, phase_scale)
    leaf_boxes = leaf_map.reshape(WIDTH, box_count, LEAF)
    blocks = basis_vector.reshape(columns, box_count, LEAF)
    coeffs = jnp.einsum("wgs,qgs->wgq", leaf_boxes, blocks, precision=highest)
    for segment_num in range(segment_count):
        coeffs = one_segment(coeffs, segment_num, group_boxes, phase_scale)
    applied = jnp.einsum("wgs,wgq->qgs", leaf_boxes, coeffs, precision=highest).reshape(
        columns, local_points
    )
    image = diagonal[None, :] * basis_vector + applied
    total_points = local_points * devices
    sketch_factor = math.sqrt(SKETCH / total_points)
    sign_values = (2 * sketch_signs - 1).astype(jnp.float32)
    block_rows = math.gcd(local_points, 512)
    block_count = local_points // block_rows
    row_blocks = sketch_rows.reshape(block_count, block_rows)
    sketch_ids = jnp.arange(SKETCH, dtype=jnp.int32)
    inner_sum, square_sum = (
        one_axis_at_a_time(jnp.sum(basis_vector * image, axis=1), BOX),
        one_axis_at_a_time(jnp.sum(basis_vector * basis_vector, axis=1), BOX),
    )
    projection = inner_sum / total_points / (square_sum / total_points + epsilon)
    residual = image - projection[:, None] * basis_vector
    energy_sum = one_axis_at_a_time(jnp.sum(residual * residual, axis=1), BOX)
    spread = jnp.sqrt(energy_sum / total_points + epsilon)
    new_basis = residual / spread[:, None]
    signed = (new_basis * sign_values[None, :]).reshape(columns, block_count, block_rows)
    signed = jnp.transpose(signed, (1, 0, 2))

    def add_block(total, pieces):
        piece, rows_here = pieces
        onehot = (rows_here[:, None] == sketch_ids[None, :]).astype(jnp.float32)
        return (
            total + jnp.dot(piece, onehot, precision=highest, preferred_element_type=jnp.float32),
            None,
        )

    total, unused = lax.scan(
        add_block, jnp.zeros((columns, SKETCH), jnp.float32), (signed, row_blocks)
    )
    sketch = lax.psum(total, BOX) * sketch_factor
    arnoldi = jnp.stack([projection, spread])
    return (new_basis, sketch, arnoldi)


def solution(mesh):
    torus = Mesh(mesh.devices.reshape(4, 8, 4, 2), ("box_0", "box_1", "box_2", "box_3"))
    placed = (P(None, BOX), P(BOX), P(None, BOX), P(), P(BOX), P(BOX))
    return jax.shard_map(
        body, mesh=torus, in_specs=placed, out_specs=(P(None, BOX), P(), P()), check_vma=False
    )
```

profile of v0, /device:TPU:1, one launch (start us, length us, event | category | flops | bytes accessed | tf_op | source)
XLA Modules:
  0.0 642.4 jit_solution(368438935068808877)
XLA Ops:
  33.5 14.7 %fusion.13 = f32[128,16,32]{2,1,0:T(8,128)} fusion(f32[32,128,16]{0,2,1:T(8,128)S(1)} %fusion.180, s32[128]{0:T(128)} %and_select_fusion.14, s32[32,32]{1,0:T(8,128)S(1)} %get-tuple-element.75, f32[32,32]{1,0:T(8,128)} %fusion.364), kind=kOutput, calls=%fused_computation.30 | convolution fusion | flops 26607616 | bytes 532992 | tf_op jit(solution)/shard_map/wvg,vgq->wgq/dot_general | solution.py:59
  50.6 13.4 %fusion.231 = f32[32,128,16]{0,2,1:T(8,128)S(1)} fusion(f32[128,16,32]{2,1,0:T(8,128)} %fusion.13, f32[32,128,16]{0,2,1:T(8,128)} %copy.19, s32[32,32]{1,0:T(8,128)} %get-tuple-element.74, s32[128]{0:T(128)} %and_select_fusion.14), kind=kOutput, calls=%fused_computation.198 | convolution fusion | flops 26673152 | bytes 791040 | tf_op jit(solution)/shard_map/wvg,vgq->wgq/dot_general | solution.py:59
  65.1 14.7 %fusion.26 = f32[128,16,32]{2,1,0:T(8,128)} fusion(f32[32,128,16]{0,2,1:T(8,128)S(1)} %fusion.231, s32[128]{0:T(128)} %and_select_fusion.12, s32[32,32]{1,0:T(8,128)} %copy-done.3, f32[32,32]{1,0:T(8,128)} %fusion.364), kind=kOutput, calls=%fused_computation.41 | convolution fusion | flops 26607616 | bytes 532992 | tf_op jit(solution)/shard_map/wvg,vgq->wgq/dot_general | solution.py:59
  82.2 13.3 %fusion.225 = f32[32,128,16]{0,2,1:T(8,128)S(1)} fusion(f32[128,16,32]{2,1,0:T(8,128)} %fusion.26, f32[32,128,16]{0,2,1:T(8,128)} %copy.21, s32[128]{0:T(128)} %and_select_fusion.12, s32[32,32]{1,0:T(8,128)} %get-tuple-element.74), kind=kOutput, calls=%fused_computation.196 | convolution fusion | flops 26673152 | bytes 791040 | tf_op jit(solution)/shard_map/wvg,vgq->wgq/dot_general | solution.py:59
  98.9 14.7 %fusion.39 = f32[128,16,32]{2,1,0:T(8,128)} fusion(f32[32,128,16]{0,2,1:T(8,128)S(1)} %fusion.225, s32[128]{0:T(128)} %and_select_fusion.10, s32[32,32]{1,0:T(8,128)} %copy-done.3, f32[32,32]{1,0:T(8,128)} %fusion.364), kind=kOutput, calls=%fused_computation.52 | convolution fusion | flops 26607616 | bytes 532992 | tf_op jit(solution)/shard_map/wvg,vgq->wgq/dot_general | solution.py:59
  116.0 13.3 %fusion.219 = f32[32,128,16]{0,2,1:T(8,128)S(1)} fusion(f32[128,16,32]{2,1,0:T(8,128)} %fusion.39, f32[32,128,16]{0,2,1:T(8,128)} %copy.23, s32[128]{0:T(128)} %and_select_fusion.10, s32[32,32]{1,0:T(8,128)} %get-tuple-element.74), kind=kOutput, calls=%fused_computation.194 | convolution fusion | flops 26673152 | bytes 791040 | tf_op jit(solution)/shard_map/wvg,vgq->wgq/dot_general | solution.py:59
  132.1 14.7 %fusion.52 = f32[128,16,32]{2,1,0:T(8,128)} fusion(f32[32,128,16]{0,2,1:T(8,128)S(1)} %fusion.219, s32[128]{0:T(128)} %and_select_fusion.8, s32[32,32]{1,0:T(8,128)} %copy-done.3, f32[32,32]{1,0:T(8,128)} %fusion.364), kind=kOutput, calls=%fused_computation.63 | convolution fusion | flops 26607616 | bytes 532992 | tf_op jit(solution)/shard_map/wvg,vgq->wgq/dot_general | solution.py:59
  149.2 13.3 %fusion.213 = f32[32,128,16]{0,2,1:T(8,128)S(1)} fusion(f32[128,16,32]{2,1,0:T(8,128)} %fusion.52, f32[32,128,16]{0,2,1:T(8,128)} %copy.25, s32[128]{0:T(128)} %and_select_fusion.8, s32[32,32]{1,0:T(8,128)} %get-tuple-element.74), kind=kOutput, calls=%fused_computation.192 | convolution fusion | flops 26673152 | bytes 791040 | tf_op jit(solution)/shard_map/wvg,vgq->wgq/dot_general | solution.py:59
  167.1 14.7 %fusion.65 = f32[128,16,32]{2,1,0:T(8,128)} fusion(f32[32,128,16]{0,2,1:T(8,128)S(1)} %fusion.213, s32[128]{0:T(128)} %and_select_fusion.6, s32[32,32]{1,0:T(8,128)} %copy-done.3, f32[32,32]{1,0:T(8,128)} %fusion.364), kind=kOutput, calls=%fused_computation.74 | convolution fusion | flops 26607616 | bytes 532992 | tf_op jit(solution)/shard_map/wvg,vgq->wgq/dot_general | solution.py:59
  184.2 13.3 %fusion.207 = f32[32,128,16]{0,2,1:T(8,128)S(1)} fusion(f32[128,16,32]{2,1,0:T(8,128)} %fusion.65, f32[32,128,16]{0,2,1:T(8,128)} %copy.27, s32[128]{0:T(128)} %and_select_fusion.6, s32[32,32]{1,0:T(8,128)} %get-tuple-element.74), kind=kOutput, calls=%fused_computation.190 | convolution fusion | flops 26673152 | bytes 791040 | tf_op jit(solution)/shard_map/wvg,vgq->wgq/dot_general | solution.py:59
  202.9 14.7 %fusion.78 = f32[128,16,32]{2,1,0:T(8,128)} fusion(f32[32,128,16]{0,2,1:T(8,128)S(1)} %fusion.207, s32[128]{0:T(128)} %and_select_fusion.4, s32[32,32]{1,0:T(8,128)} %copy-done.3, f32[32,32]{1,0:T(8,128)} %fusion.364), kind=kOutput, calls=%fused_computation.85 | convolution fusion | flops 26607616 | bytes 532992 | tf_op jit(solution)/shard_map/wvg,vgq->wgq/dot_general | solution.py:59
  220.0 13.3 %fusion.201 = f32[32,128,16]{0,2,1:T(8,128)S(1)} fusion(f32[128,16,32]{2,1,0:T(8,128)} %fusion.78, f32[32,128,16]{0,2,1:T(8,128)} %copy.29, s32[128]{0:T(128)} %and_select_fusion.4, s32[32,32]{1,0:T(8,128)} %get-tuple-element.74), kind=kOutput, calls=%fused_computation.188 | convolution fusion | flops 26673152 | bytes 791040 | tf_op jit(solution)/shard_map/wvg,vgq->wgq/dot_general | solution.py:59
  236.0 14.7 %fusion.91 = f32[128,16,32]{2,1,0:T(8,128)} fusion(f32[32,128,16]{0,2,1:T(8,128)S(1)} %fusion.201, s32[128]{0:T(128)} %and_select_fusion.2, s32[32,32]{1,0:T(8,128)} %copy-done.3, f32[32,32]{1,0:T(8,128)} %fusion.364), kind=kOutput, calls=%fused_computation.96 | convolution fusion | flops 26607616 | bytes 532992 | tf_op jit(solution)/shard_map/wvg,vgq->wgq/dot_general | solution.py:59
  253.1 13.3 %fusion.195 = f32[32,128,16]{0,2,1:T(8,128)S(1)} fusion(f32[128,16,32]{2,1,0:T(8,128)} %fusion.91, f32[32,128,16]{0,2,1:T(8,128)} %copy.31, s32[128]{0:T(128)} %and_select_fusion.2, s32[32,32]{1,0:T(8,128)} %get-tuple-element.74), kind=kOutput, calls=%fused_computation.186 | convolution fusion | flops 26673152 | bytes 791040 | tf_op jit(solution)/shard_map/wvg,vgq->wgq/dot_general | solution.py:59
  270.2 14.7 %fusion.104 = f32[128,16,32]{2,1,0:T(8,128)} fusion(f32[32,128,16]{0,2,1:T(8,128)S(1)} %fusion.195, s32[128]{0:T(128)} %and_select_fusion, s32[32,32]{1,0:T(8,128)} %copy-done.3, f32[32,32]{1,0:T(8,128)} %fusion.364), kind=kOutput, calls=%fused_computation.107 | convolution fusion | flops 26607616 | bytes 532992 | tf_op jit(solution)/shard_map/wvg,vgq->wgq/dot_general | solution.py:59
  286.4 14.2 %fusion.189 = f32[32,128,16]{0,2,1:T(8,128)S(1)} fusion(f32[128,16,32]{2,1,0:T(8,128)} %fusion.104, f32[32,128,16]{0,2,1:T(8,128)S(1)} %copy.33, s32[128]{0:T(128)} %and_select_fusion, s32[32,32]{1,0:T(8,128)} %get-tuple-element.74), kind=kOutput, calls=%fused_computation.184 | convolution fusion | flops 26673152 | bytes 791040 | tf_op jit(solution)/shard_map/wvg,vgq->wgq/dot_general | solution.py:59
  309.8 11.4 %all-reduce = (f32[16]{0:T(128)S(1)}, f32[16]{0:T(128)S(1)}) all-reduce(f32[16]{0:T(128)S(1)} %get-tuple-element.64, f32[16]{0:T(128)S(1)} %get-tuple-element.65), channel_id=1, replica_groups=mesh['box_0'=4,'box_1'=8,'box_2'=4,'box_3'=2] {'box_1'}, use_global_device_ids=true, to_apply=%region_7.8 | all-reduce | flops 32 | bytes 256 | tf_op jit(solution)/shard_map/psum | solution.py:26
  327.3 11.8 %all-reduce.3 = (f32[16]{0:T(128)S(1)}, f32[16]{0:T(128)S(1)}) all-reduce(f32[16]{0:T(128)S(1)} %get-tuple-element.62, f32[16]{0:T(128)S(1)} %get-tuple-element.63), channel_id=1, replica_groups=mesh['box_0'=4,'box_1'=8,'box_2'=4,'box_3'=2] {'box_3'}, use_global_device_ids=true, to_apply=%region_9.10 | all-reduce | flops 32 | bytes 256 | tf_op jit(solution)/shard_map/psum | solution.py:26
  339.4 7.5 %psum.99 = f32[16]{0:T(128)S(1)} all-reduce(f32[16]{0:T(128)S(1)} %multiply_reduce_fusion), channel_id=1, replica_groups=mesh['box_0'=4,'box_1'=8,'box_2'=4,'box_3'=2] {'box_0'}, use_global_device_ids=true, to_apply=%region_11.12 | all-reduce | flops 16 | bytes 128 | tf_op jit(solution)/shard_map/psum | solution.py:26
  346.9 11.4 %psum.100 = f32[16]{0:T(128)S(1)} all-reduce(f32[16]{0:T(128)S(1)} %psum.99), channel_id=1, replica_groups=mesh['box_0'=4,'box_1'=8,'box_2'=4,'box_3'=2] {'box_1'}, use_global_device_ids=true, to_apply=%region_12.13 | all-reduce | flops 16 | bytes 128 | tf_op jit(solution)/shard_map/psum | solution.py:26
  358.3 7.2 %psum.101 = f32[16]{0:T(128)S(1)} all-reduce(f32[16]{0:T(128)S(1)} %psum.100), channel_id=1, replica_groups=mesh['box_0'=4,'box_1'=8,'box_2'=4,'box_3'=2] {'box_2'}, use_global_device_ids=true, to_apply=%region_13.14 | all-reduce | flops 16 | bytes 128 | tf_op jit(solution)/shard_map/psum | solution.py:26
  365.5 10.2 %psum.102 = f32[16]{0:T(128)S(1)} all-reduce(f32[16]{0:T(128)S(1)} %psum.101), channel_id=1, replica_groups=mesh['box_0'=4,'box_1'=8,'box_2'=4,'box_3'=2] {'box_3'}, use_global_device_ids=true, to_apply=%region_14.15 | all-reduce | flops 16 | bytes 128 | tf_op jit(solution)/shard_map/psum | solution.py:26
  376.6 17.6 %while.11 = (s32[]{:T(128)}, f32[16,2048]{1,0:T(8,128)S(1)}, f32[8,16,512]{2,1,0:T(8,128)S(1)}, s32[8,512]{1,0:T(8,128)}, s32[]{:T(128)}, /*index=5*/s32[]{:T(128)}) while((s32[]{:T(128)}, f32[16,2048]{1,0:T(8,128)S(1)}, f32[8,16,512]{2,1,0:T(8,128)S(1)}, s32[8,512]{1,0:T(8,128)}, s32[]{:T(128)}, /*index=5*/s32[]{:T(128)}) %tuple.39), condition=%wide.region_16.17_spmd.clone, body=%wide.region_15.16_spmd.clone.sunk | while | flops 202440704 | bytes 301151 | solution.py:114
  395.5 238.3 %all-reduce.6.cloned.1.call-done = f32[16,2048]{1,0:T(8,128)} async-done(((f32[16,2048]{1,0:T(8,128)}), f32[16,2048]{1,0:T(8,128)}) %all-reduce.6.cloned.1.call-update) | async-done | bytes 131088 | tf_op jit(solution)/shard_map/psum | solution.py:117
  (97 shorter events, 104.5 us)
Async XLA Ops:
  7.2 626.6 %all-reduce.6.cloned.1.call-start = ((), (), s32[]{:S(2)}) async-start(), calls=%async_computation | async-start | bytes 262144 | tf_op jit(solution)/shard_map/psum | solution.py:117
  9.1 3.3 copy-start
  20.0 28.2 %collective-permute-start = (f32[32,128,16]{1,2,0:T(8,128)}, f32[32,128,16]{1,2,0:T(8,128)}, u32[]{:S(2)}, u32[]{:S(2)}) collective-permute-start(f32[32,128,16]{1,2,0:T(8,128)} %copy.18), channel_id=1, source_target_pairs={{0,1},{1,0},{2,3},{3,2},{4,5},{5,4},{6,7},{7,6},{8,9},{9,8},{10,11... | collective-permute-start | bytes 786440 | tf_op jit(solution)/shard_map/ppermute | solution.py:22
  33.5 14.7 %copy-start.3 = (s32[32,32]{1,0:T(8,128)}, s32[32,32]{1,0:T(8,128)S(1)}, u32[]{:S(2)}) copy-start(s32[32,32]{1,0:T(8,128)S(1)} %get-tuple-element.75) | copy-start | bytes 12292
  65.1 14.7 %collective-permute-start.1 = (f32[32,128,16]{1,2,0:T(8,128)}, f32[32,128,16]{1,2,0:T(8,128)}, u32[]{:S(2)}, u32[]{:S(2)}) collective-permute-start(f32[32,128,16]{1,2,0:T(8,128)} %copy.20), channel_id=1, source_target_pairs={{0,2},{1,3},{2,0},{3,1},{4,6},{5,7},{6,4},{7,5},{8,10},{9,11},{10,... | collective-permute-start | bytes 786440 | tf_op jit(solution)/shard_map/ppermute | solution.py:22
  96.8 16.8 %collective-permute-start.2 = (f32[32,128,16]{1,2,0:T(8,128)}, f32[32,128,16]{1,2,0:T(8,128)}, u32[]{:S(2)}, u32[]{:S(2)}) collective-permute-start(f32[32,128,16]{1,2,0:T(8,128)} %copy.22), channel_id=1, source_target_pairs={{0,4},{1,5},{2,6},{3,7},{4,0},{5,1},{6,2},{7,3},{8,12},{9,13},{10,... | collective-permute-start | bytes 786440 | tf_op jit(solution)/shard_map/ppermute | solution.py:22
  130.5 16.3 %collective-permute-start.3 = (f32[32,128,16]{1,2,0:T(8,128)}, f32[32,128,16]{1,2,0:T(8,128)}, u32[]{:S(2)}, u32[]{:S(2)}) collective-permute-start(f32[32,128,16]{1,2,0:T(8,128)} %copy.24), channel_id=1, source_target_pairs={{0,8},{1,9},{2,10},{3,11},{4,12},{5,13},{6,14},{7,15},{8,0},{9,1},... | collective-permute-start | bytes 786440 | tf_op jit(solution)/shard_map/ppermute | solution.py:22
  163.7 18.1 %collective-permute-start.4 = (f32[32,128,16]{1,2,0:T(8,128)}, f32[32,128,16]{1,2,0:T(8,128)}, u32[]{:S(2)}, u32[]{:S(2)}) collective-permute-start(f32[32,128,16]{1,2,0:T(8,128)} %copy.26), channel_id=1, source_target_pairs={{0,16},{1,17},{2,18},{3,19},{4,20},{5,21},{6,22},{7,23},{8,24},{9,... | collective-permute-start | bytes 786440 | tf_op jit(solution)/shard_map/ppermute | solution.py:22
  198.7 18.9 %collective-permute-start.5 = (f32[32,128,16]{1,2,0:T(8,128)}, f32[32,128,16]{1,2,0:T(8,128)}, u32[]{:S(2)}, u32[]{:S(2)}) collective-permute-start(f32[32,128,16]{1,2,0:T(8,128)} %copy.28), channel_id=1, source_target_pairs={{0,32},{1,33},{2,34},{3,35},{4,36},{5,37},{6,38},{7,39},{8,40},{9,... | collective-permute-start | bytes 786440 | tf_op jit(solution)/shard_map/ppermute | solution.py:22
  234.6 16.1 %collective-permute-start.6 = (f32[32,128,16]{1,2,0:T(8,128)}, f32[32,128,16]{1,2,0:T(8,128)}, u32[]{:S(2)}, u32[]{:S(2)}) collective-permute-start(f32[32,128,16]{1,2,0:T(8,128)} %copy.30), channel_id=1, source_target_pairs={{0,64},{1,65},{2,66},{3,67},{4,68},{5,69},{6,70},{7,71},{8,72},{9,... | collective-permute-start | bytes 786440 | tf_op jit(solution)/shard_map/ppermute | solution.py:22
  267.6 17.3 %collective-permute-start.7 = (f32[32,128,16]{1,2,0:T(8,128)}, f32[32,128,16]{1,2,0:T(8,128)}, u32[]{:S(2)}, u32[]{:S(2)}) collective-permute-start(f32[32,128,16]{1,2,0:T(8,128)} %copy.32), channel_id=1, source_target_pairs={{0,128},{1,129},{2,130},{3,131},{4,132},{5,133},{6,134},{7,135},{8... | collective-permute-start | bytes 786440 | tf_op jit(solution)/shard_map/ppermute | solution.py:22
  302.7 0.9 copy-start.1
  394.2 0.7 copy-start.2
Sparse Core Ops, SparseCore 0:
  395.0 238.7 all-reduce.5
where the time goes:
time: 651 us; the launch traced here: 642 us
  matrix products  244 us (37%)
  waiting for transfers between devices  238 us (37%)
  blocking collectives  71.8 us (11%)
  local copies, waits for them, and re-layouts  40.7 us (6%)
  starting transfers between devices  19.1 us (3%)
  between operations  15.1 us (2%)
  other arithmetic  13.4 us (2%)
    psum x1, waiting for transfers between devices, body(): sketch = lax.psum(total, BOX) * sketch_factor  238 us
    dot_general x16, matrix products, mix(): jnp.einsum('wvg,vgq->wgq', matrix, coeffs, precision=lax.Precision.HIGHEST)  225 us
    psum x8, blocking collectives, one_axis_at_a_time(): return functools.reduce(lax.psum, axes, x)  71.8 us
    ppermute x8, starting transfers between devices, swapped(): lax.ppermute(x, axis, [(i, i ^ 1 << bit) for i in range(lax.axis_size(axi...  19 us
    ppermute x8, local copies, waits for them, and re-layouts, swapped(): lax.ppermute(x, axis, [(i, i ^ 1 << bit) for i in range(lax.axis_size(axi...  18.3 us
  transfers between devices with their start and end apart: 9, of which 1 were waited for; matrix products, arithmetic and copies ran while one was open for 20% of the time, Pallas kernels for 0%

commit v1 on v0

v1 whole, which is shorter than its diff:
```python
import functools
import math

import jax
import jax.numpy as jnp
from jax import lax
from jax.experimental import pallas as pl
from jax.experimental.pallas import tpu as pltpu
from jax.sharding import Mesh
from jax.sharding import PartitionSpec as P

RANK = 16
WIDTH = 32
LEAF = 32
SKETCH = 2048
NRHS = 16
SECTIONS = 8
CHIPS = 128
NPTS = 1048576
MOD = 8191
EPS = 1e-06
CHIP = ("box_0", "box_1", "box_2")
CORE = "box_3"
FORWARD = 6
BACK = 9
F32 = jnp.float32


def fold(x):
    return (x & MOD) + (x >> 13)


def unit_circle(phase):
    r = phase.astype(F32)
    r = jnp.where(r > 4095.5, r - float(MOD), r)
    y = r * (math.pi / MOD)
    y2 = y * y
    s = 1.0 / math.factorial(13)
    for k in (11, 9, 7, 5, 3, 1):
        s = s * y2 + (-1.0) ** (k // 2) / math.factorial(k)
    s = s * y
    c = -1.0 / math.factorial(14)
    for k in (12, 10, 8, 6, 4, 2, 0):
        c = c * y2 + (-1.0) ** (k // 2) / math.factorial(k)
    return 1.0 - 2.0 * s * s, 2.0 * s * c


def times(a, b):
    return a[0] * b[0] - a[1] * b[1], a[0] * b[1] + a[1] * b[0]


def pack_kernel(v_ref, coords_ref, diag_ref, rows_ref, signs_ref, out_ref, turned):
    zeros = jnp.zeros((11, 128), F32)
    for jb in range(8):
        tiles = []
        for jt in range(4):
            cols = pl.ds((jb * 4 + jt) * 128, 128)
            tiles += [
                v_ref[:, cols],
                coords_ref[:, cols].astype(F32),
                diag_ref[:, cols],
                rows_ref[:, cols].astype(F32),
                signs_ref[:, cols].astype(F32),
                zeros,
            ]
        turned[pl.ds(jb * 128, 128), :] = jnp.concatenate(tiles, 0).T
    lane = lax.broadcasted_iota(jnp.int32, (32, 128), 1)
    for jt in range(4):
        made = {}
        for s in range(LEAF):
            rows = turned[pl.ds(s, 32, stride=32), :]
            for col, start, width, at in (
                (s // 8, jt * 32, 16, 16 * (s % 8)),
                (4 + s // 16, jt * 32 + 16, 8, 8 * (s % 16)),
            ):
                shift = (at - start) % 128
                moved = pltpu.roll(rows, shift, 1) if shift else rows
                if col in made:
                    moved = jnp.where(lane >= at, moved, made[col])
                made[col] = moved
        for col in range(FORWARD):
            out_ref[pl.ds(jt * 32 * FORWARD + col, 32, stride=FORWARD), :] = made[col]


def product(out_count, terms, store, start=None):
    def tile(t, carry):
        accs = [None] * 8
        if start is not None:
            accs = [start(t * 8 + i) for i in range(8)]
        for matrix, vector in terms:
            for b in range(32):
                vec = vector(b)
                for i in range(8):
                    term = matrix(t * 8 + i, b) * vec
                    accs[i] = term if accs[i] is None else accs[i] + term
        for i in range(8):
            store(t * 8 + i, accs[i])
        return carry

    lax.fori_loop(0, out_count // 8, tile, 0)


def row16(a):
    return pl.ds(pl.multiple_of(a * 16, 16), 16)


def leaf_kernel(info_ref, got_ref, coeffs_ref, leaf_ref, points_ref):
    for c in range(FORWARD):
        points_ref[pl.ds(c * 128, 128), :] = got_ref[pl.ds(c, 128, stride=FORWARD), :].T
    scale = info_ref[0]

    def powers(field):
        where = points_ref[pl.ds(512 + field, 32, stride=8), :].astype(jnp.int32)
        one = unit_circle(fold(fold(where * scale)))
        two = times(one, one)
        return [one, two, times(two, one), times(two, two)]

    first, second = powers(0), powers(1)
    gain = 1.0 / math.sqrt(LEAF)
    second = [(c * gain, s * gain) for c, s in second]
    for w in range(RANK):
        c, s = times(first[w % 4], second[w // 4])
        leaf_ref[w] = c
        leaf_ref[w + RANK] = s

    def store(a, x):
        coeffs_ref[row16(a), :] = x

    product(
        WIDTH,
        [(lambda a, b: leaf_ref[a, b : b + 1, :], lambda b: points_ref[pl.ds(b * 16, 16), :])],
        store,
    )


def section_map(map_ref, unit, offset, first_power, turn, gain):
    index = lax.broadcasted_iota(jnp.int32, (WIDTH, 128), 0) + offset
    one = unit_circle(fold(fold(unit * index)))
    two = times(one, one)
    four = times(two, two)
    scale = (gain * math.cos(turn), gain * math.sin(turn))
    power = one if first_power == 1 else times(two, one)
    power = (
        power[0] * scale[0] - power[1] * scale[1],
        power[0] * scale[1] + power[1] * scale[0],
    )
    fine = [power]
    for _ in range(3):
        fine.append(times(fine[-1], one))
    coarse = None
    for i in range(8):
        for j in range(4):
            c, s = fine[j]
            map_ref[4 * i + j] = c if coarse is None else coarse[0] * c - coarse[1] * s
        coarse = four if coarse is None else times(coarse, four)


def state_rows(parts):
    pad = [jnp.zeros((128 - 16 * len(parts), 128), F32)]
    return jnp.sum(jnp.concatenate(parts + pad, 0).T, axis=0, keepdims=True)


def core_kernel(
    info_ref,
    coeffs_ref,
    partner_ref,
    leaf_ref,
    points_ref,
    out_ref,
    now,
    other,
    later,
    own_map,
    cross_map,
    image,
    high,
    low,
    lhs,
    rhs,
):
    scale, chip, core = info_ref[0], info_ref[1], info_ref[2]
    place = ((chip >> 2) & 7) * 16 + (chip >> 5) * 4 + (chip & 3)
    lane = lax.broadcasted_iota(jnp.int32, (1, 128), 1)
    box = (lane * 2 + core) * 128 + place
    now[...] = coeffs_ref[...]
    other[...] = partner_ref[...]
    lanes = lax.broadcasted_iota(jnp.int32, (NRHS, 128), 1)

    def section(k, carry):
        key = box * 37 + 101 * k
        whole = (key.astype(F32) * (1.0 / (MOD - 1))).astype(jnp.int32)
        key = key - whole * (MOD - 1)
        key = jnp.where(key < 0, key + (MOD - 1), key)
        key = jnp.where(key >= MOD - 1, key - (MOD - 1), key)
        unit = fold(fold((key + 1) * scale))
        section_map(own_map, unit, 2, 1, 0.0, 0.35 / math.sqrt(WIDTH))
        section_map(cross_map, unit, 1, 3, 2.0 * math.pi * 4096 / MOD, 0.6 / math.sqrt(WIDTH))

        def store(a, x):
            later[row16(a), :] = x

        product(
            WIDTH,
            [
                (lambda a, b: own_map[a, b : b + 1, :], lambda b: now[pl.ds(b * 16, 16), :]),
                (lambda a, b: cross_map[a, b : b + 1, :], lambda b: other[pl.ds(b * 16, 16), :]),
            ],
            store,
            lambda a: 0.85 * now[row16(a), :],
        )
        step = jnp.left_shift(1, jnp.minimum(k, SECTIONS - 2))
        bit = (lanes & step) == 0
        for a in range(WIDTH):
            x = later[pl.ds(a * 16, 16), :]
            now[pl.ds(a * 16, 16), :] = x
            other[pl.ds(a * 16, 16), :] = jnp.where(
                bit, pltpu.roll(x, 128 - step, 1), pltpu.roll(x, step, 1)
            )
        return carry

    lax.fori_loop(0, SECTIONS, section, 0)

    rows = points_ref[pl.ds(512 + 3, 32, stride=8), :].astype(jnp.int32)
    high[...] = rows >> 8
    low[...] = rows & 255
    square = jnp.zeros((NRHS, 128), F32)
    inner = jnp.zeros((NRHS, 128), F32)
    for t in range(4):
        accs = [None] * 8
        for w in range(WIDTH):
            vec = now[pl.ds(w * 16, 16), :]
            for i in range(8):
                s = t * 8 + i
                term = leaf_ref[w, s : s + 1, :] * vec
                accs[i] = term if accs[i] is None else accs[i] + term
        for i in range(8):
            s = t * 8 + i
            v = points_ref[pl.ds(s * 16, 16), :]
            x = points_ref[pl.ds(512 + s * 8 + 2, 1), :] * v + accs[i]
            image[pl.ds(s * 16, 16), :] = x
            square += v * v
            inner += v * x
    sums = state_rows([square, inner])
    valid = lane < 16
    vv = jnp.where(valid, sums, 0.0)
    iv = jnp.where(valid, pltpu.roll(sums, 112, 1), 0.0)
    local = jnp.where(vv > 0.0, iv / jnp.where(vv > 0.0, vv, 1.0), 0.0)
    across = jnp.broadcast_to(local, (128, 128)).T[0:NRHS, :]
    energy = jnp.zeros((NRHS, 128), F32)
    mixed = jnp.zeros((NRHS, 128), F32)
    hot = lax.broadcasted_iota(jnp.int32, (256, 128), 0)
    for s in range(LEAF):
        v = points_ref[pl.ds(s * 16, 16), :]
        x = image[pl.ds(s * 16, 16), :]
        r = x - across * v
        energy += r * r
        mixed += r * v
        sign = 2.0 * points_ref[pl.ds(512 + s * 8 + 4, 1), :] - 1.0
        parts = []
        for y in (x * sign, v * sign):
            top = y.astype(jnp.bfloat16).astype(F32)
            parts.append((top, y - top))
        which = high[s : s + 1, :]
        cols = pl.ds(s * 128, 128)
        for h in range(8):
            mask = jnp.broadcast_to(which == h, (NRHS, 128))
            for p in range(2):
                for c in range(2):
                    lhs[pl.ds(p * 256 + h * 32 + c * 16, 16), cols] = jnp.where(
                        mask, parts[c][p], 0.0
                    ).astype(jnp.bfloat16)
        rhs[:, cols] = jnp.where(hot == low[s : s + 1, :], 1.0, 0.0).astype(jnp.bfloat16)
    spread_out = lax.dot_general(
        lhs[...], rhs[...], (((1,), (1,)), ((), ())), preferred_element_type=F32
    )
    spread_out = spread_out[0:256] + spread_out[256:512]
    for c in range(4):
        out_ref[pl.ds(c, 128, stride=BACK), :] = image[pl.ds(c * 128, 128), :].T
    for c in range(2):
        for half in range(2):
            tile = jnp.concatenate(
                [
                    spread_out[
                        (t // 2) * 32 + c * 16 : (t // 2) * 32 + c * 16 + 16,
                        (t % 2) * 128 : (t % 2) * 128 + 128,
                    ]
                    for t in range(half * 8, half * 8 + 8)
                ],
                0,
            )
            out_ref[pl.ds(4 + c * 2 + half, 128, stride=BACK), :] = tile.T
    rest = jnp.where(lane < 32, state_rows([energy, mixed]), 0.0)
    state = vv + pltpu.roll(local, 16, 1) + pltpu.roll(rest, 32, 1)
    out_ref[pl.ds(8, 128, stride=BACK), :] = jnp.broadcast_to(state, (128, 128))


def merged(vv, p, e, cr, total):
    square = total(vv)
    inner = total(p * vv + cr)
    local = jnp.where(square > 0.0, inner / jnp.where(square > 0.0, square, 1.0), 0.0)
    return square, inner, local


def moved_energy(vv, p, e, cr, at, total):
    off = p - at
    return total(e + off * (2.0 * cr + off * vv)), total(cr + off * vv)


def sum_kernel(got_ref, out_ref):
    for c in range(4):
        out_ref[c : c + 1, :] = jnp.sum(
            got_ref[pl.ds(4 + c, 128, stride=BACK), :], axis=0, keepdims=True
        )
    state = got_ref[pl.ds(8, 128, stride=BACK), :]
    valid = lax.broadcasted_iota(jnp.int32, (128, 128), 1) < 16
    parts = [
        jnp.where(valid, pltpu.roll(state, (128 - 16 * i) % 128, 1) if i else state, 0.0)
        for i in range(4)
    ]

    def total(x):
        return jnp.sum(x, axis=0, keepdims=True)

    square, inner, local = merged(*parts, total)
    energy, mixed = moved_energy(*parts, local, total)
    for i, x in enumerate((square, local, energy, mixed)):
        out_ref[4 + i : 5 + i, :] = x


def finish_kernel(got_ref, mine_ref, theirs_ref, v_ref, basis_ref, chunk_ref, arnoldi_ref, turned):
    both = [(mine_ref[4 + i : 5 + i, :], theirs_ref[4 + i : 5 + i, :]) for i in range(4)]
    vv, p, e, cr = both
    square = vv[0] + vv[1]
    inner = (p[0] * vv[0] + cr[0]) + (p[1] * vv[1] + cr[1])
    proj = (inner / NPTS) / (square / NPTS + EPS)
    terms = []
    for i in range(2):
        off = p[i] - proj
        terms.append(e[i] + off * (2.0 * cr[i] + off * vv[i]))
    spread = jnp.sqrt(jnp.maximum(terms[0] + terms[1], 0.0) / NPTS + EPS)
    arnoldi_ref[0:1, :] = proj[:, 0:NRHS]
    arnoldi_ref[1:2, :] = spread[:, 0:NRHS]
    valid = lax.broadcasted_iota(jnp.int32, (1, 128), 1) < 16

    def tiled(x):
        x = jnp.where(valid, x, 0.0)
        for shift in (16, 32, 64):
            x = x + pltpu.roll(x, shift, 1)
        return x

    proj, spread = tiled(proj), tiled(spread)
    sums = mine_ref[0:4, :] + theirs_ref[0:4, :]
    chunk = (sums[0:2] - proj * sums[2:4]) / spread * math.sqrt(SKETCH / NPTS)
    for i in range(2):
        chunk_ref[pl.ds(i, 128, stride=2), :] = jnp.broadcast_to(chunk[i : i + 1], (128, 128))
    proj = jnp.broadcast_to(proj, (128, 128)).T[0:NRHS, :]
    spread = jnp.broadcast_to(spread, (128, 128)).T[0:NRHS, :]
    lane = lax.broadcasted_iota(jnp.int32, (32, 128), 1)
    for s in range(LEAF):
        made = None
        for jt in range(4):
            rows = got_ref[pl.ds(jt * 32 * BACK + s // 8, 32, stride=BACK), :]
            shift = (jt * 32 - (s % 8) * 16) % 128
            rows = pltpu.roll(rows, shift, 1) if shift else rows
            made = rows if made is None else jnp.where(lane >= jt * 32, rows, made)
        turned[pl.ds(s, 32, stride=32), :] = made
    for jb in range(8):
        back = turned[pl.ds(jb * 128, 128), :].T
        for jt in range(4):
            cols = pl.ds((jb * 4 + jt) * 128, 128)
            x = back[jt * 32 : jt * 32 + 16, :]
            basis_ref[:, cols] = (x - proj * v_ref[:, cols]) / spread


def spread_kernel(got_ref, out_ref):
    for half in range(2):
        tile = got_ref[pl.ds(half, 128, stride=2), :].T
        for t in range(8):
            out_ref[:, pl.ds((half * 8 + t) * 128, 128)] = tile[t * 16 : t * 16 + 16, :]


VMEM = pl.BlockSpec(memory_space=pltpu.VMEM)
SMEM = pl.BlockSpec(memory_space=pltpu.SMEM)


def f32(*shape):
    return jax.ShapeDtypeStruct(shape, F32)


def call(kernel, out, ins, scratch=(), flops=1000000):
    single = not isinstance(out, tuple)
    return pl.pallas_call(
        kernel,
        out_shape=out,
        in_specs=ins,
        out_specs=VMEM if single else tuple(VMEM for _ in out),
        scratch_shapes=list(scratch),
        cost_estimate=pl.CostEstimate(flops=flops, bytes_accessed=1000000, transcendentals=0),
        compiler_params=pltpu.CompilerParams(vmem_limit_bytes=48 * 1024 * 1024),
    )


def exchange(x, columns):
    x = lax.all_to_all(x.reshape(CHIPS, columns, 128), CHIP, 0, 0, tiled=True)
    return x.reshape(CHIPS * columns, 128)


def body(basis_vector, diagonal, coords, phase_scale, sketch_rows, sketch_signs):
    chip = lax.axis_index(CHIP)
    core = lax.axis_index(CORE)
    info = jnp.stack([phase_scale[0] % MOD, chip, core]).astype(jnp.int32)
    points = LEAF * CHIPS
    packed = call(pack_kernel, f32(CHIPS * FORWARD, 128), [VMEM] * 5, [pltpu.VMEM((1024, 128), F32)])(
        basis_vector,
        coords,
        diagonal.reshape(1, points),
        sketch_rows.reshape(1, points),
        sketch_signs.reshape(1, points),
    )
    got = exchange(packed, FORWARD)
    coeffs, leaf, held = call(
        leaf_kernel,
        (f32(512, 128), f32(WIDTH, LEAF, 128), f32(FORWARD * 128, 128)),
        [SMEM, VMEM],
    )(info, got)
    partner = lax.ppermute(coeffs, CORE, [(0, 1), (1, 0)])
    big = pltpu.VMEM((512, 128), F32)
    square = pltpu.VMEM((WIDTH, WIDTH, 128), F32)
    index = pltpu.VMEM((LEAF, 128), jnp.int32)
    back = call(
        core_kernel,
        f32(CHIPS * BACK, 128),
        [SMEM] + [VMEM] * 4,
        [
            big,
            big,
            big,
            square,
            square,
            big,
            index,
            index,
            pltpu.VMEM((512, points), jnp.bfloat16),
            pltpu.VMEM((256, points), jnp.bfloat16),
        ],
    )(info, coeffs, partner, leaf, held)
    home = exchange(back, BACK)
    mine = call(sum_kernel, f32(8, 128), [VMEM])(home)
    theirs = lax.ppermute(mine, CORE, [(0, 1), (1, 0)])
    new_basis, chunk, arnoldi = call(
        finish_kernel,
        (f32(NRHS, points), f32(CHIPS * 2, 128), f32(2, NRHS)),
        [VMEM] * 4,
        [pltpu.VMEM((1024, 128), F32)],
    )(home, mine, theirs, basis_vector)
    sketch = call(spread_kernel, f32(NRHS, SKETCH), [VMEM])(exchange(chunk, 2))
    return new_basis, sketch, arnoldi


def solution(mesh):
    torus = Mesh(mesh.devices.reshape(4, 8, 4, 2), ("box_0", "box_1", "box_2", "box_3"))
    box = ("box_0", "box_1", "box_2", "box_3")
    placed = (P(None, box), P(box), P(None, box), P(), P(box), P(box))
    return jax.shard_map(
        body, mesh=torus, in_specs=placed, out_specs=(P(None, box), P(), P()), check_vma=False
    )
```

time: 651 us -> 124 us (0.19); the launches traced: 642 us -> 123 us
  matrix products: 244 us -> 0 us
  waiting for transfers between devices: 238 us -> 18.3 us
  local copies, waits for them, and re-layouts: 40.7 us -> 4.88 us
  Pallas kernels: 0 us -> 24 us
  blocking collectives: 71.8 us -> 51.6 us
  between operations: 15.1 us -> 1.38 us
  other arithmetic: 13.4 us -> 0.08 us
    dot_general x26 -> x0, matrix products: 244 us -> none  [the longest x16 225 us: mix(): jnp.einsum('wvg,vgq->wgq', matrix, coeffs, precision=lax.Precision.HIGHEST)]
    psum x1 -> x0, waiting for transfers between devices: 238 us -> none  [body(): sketch = lax.psum(total, BOX) * sketch_factor]
    psum x8 -> x0, blocking collectives: 71.8 us -> none  [one_axis_at_a_time(): return functools.reduce(lax.psum, axes, x)]
    all_to_all x0 -> x2, blocking collectives: none -> 51.6 us  [exchange(): x = lax.all_to_all(x.reshape(CHIPS, columns, 128), CHIP, 0, 0, tiled=True)]
    pallas_call x0 -> x6, Pallas kernels: none -> 24 us  [the longest x1 18.4 us: body(): call(core_kernel, f32(CHIPS * BACK, 128), [SMEM] + [VMEM] * 4, [big, big,...]
    ppermute x8 -> x0, local copies, waits for them, and re-layouts: 18.3 us -> none  [swapped(): lax.ppermute(x, axis, [(i, i ^ 1 << bit) for i in range(lax.axis_size(axi...]
    all_to_all x0 -> x1, starting transfers between devices: none -> 16.3 us  [exchange(): x = lax.all_to_all(x.reshape(CHIPS, columns, 128), CHIP, 0, 0, tiled=True)]
    all_to_all x0 -> x1, waiting for transfers between devices: none -> 16.3 us  [exchange(): x = lax.all_to_all(x.reshape(CHIPS, columns, 128), CHIP, 0, 0, tiled=True)]
  transfers between devices with their start and end apart: 9 -> 3, of which waited for: 1 -> 3; matrix products, arithmetic and copies ran while one was open for 20% -> 0% of each run, Pallas kernels for 0% -> 0%
where the time goes in v1:
time: 124 us; the launch traced here: 123 us
  blocking collectives  51.6 us (42%)
  Pallas kernels  24 us (19%)
  starting transfers between devices  23.3 us (19%)
  waiting for transfers between devices  18.3 us (15%)
  local copies, waits for them, and re-layouts  4.88 us (4%)
  between operations  1.38 us (1%)
    all_to_all x2, blocking collectives, exchange(): x = lax.all_to_all(x.reshape(CHIPS, columns, 128), CHIP, 0, 0, tiled=True)  51.6 us
    pallas_call x1, Pallas kernels, body(): call(core_kernel, f32(CHIPS * BACK, 128), [SMEM] + [VMEM] * 4, [big, big,...  18.4 us
    all_to_all x1, starting transfers between devices, exchange(): x = lax.all_to_all(x.reshape(CHIPS, columns, 128), CHIP, 0, 0, tiled=True)  16.3 us
    all_to_all x1, waiting for transfers between devices, exchange(): x = lax.all_to_all(x.reshape(CHIPS, columns, 128), CHIP, 0, 0, tiled=True)  16.3 us
    unnamed x12, local copies, waits for them, and re-layouts  3.86 us
    ppermute x1, starting transfers between devices, body(): theirs = lax.ppermute(mine, CORE, [(0, 1), (1, 0)])  3.53 us
    ppermute x1, starting transfers between devices, body(): partner = lax.ppermute(coeffs, CORE, [(0, 1), (1, 0)])  3.44 us
  transfers between devices with their start and end apart: 3, of which 3 were waited for; matrix products, arithmetic and copies ran while one was open for 0% of the time, Pallas kernels for 0%

profile of v1, /device:TPU:1, one launch (start us, length us, event | category | flops | bytes accessed | tf_op | source)
XLA Modules:
  0.0 123.5 jit_solution(11065451989831593259)
XLA Ops:
  0.6 0.9 copy-done
  1.6 0.8 copy-done.2
  2.3 0.7 copy-done.3
  3.1 0.7 copy-done.4
  3.8 0.7 copy-done.5
  4.5 1.5 %shard_map.85 = f32[768,128]{1,0:T(8,128)S(1)} custom-call(f32[16,4096]{1,0:T(8,128)S(1)} %copy-done, s32[2,4096]{1,0:T(2,128)S(1)} %copy-done.2, f32[1,4096]{1,0:T(1,128)S(1)} %bitcast.11, s32[1,4096]{1,0:T(1,128)S(1)} %bitcast.12, s32[1,4096]{1,0:T(1,128)S(1)} %bitcast.13), custom_call_target="tpu_custom_call" | custom-call | flops 1000000 | bytes 1000000 | tf_op jit(solution)/shard_map/pallas_call | solution.py:413
  6.0 0.8 reshape.38
  6.8 16.3 %all-to-all-start = ((f32[128,6,128]{2,1,0:T(8,128)}), f32[128,6,128]{2,1,0:T(8,128)S(1)}, u32[]{:S(2)}, u32[]{:S(2)}) async-start(f32[128,6,128]{2,1,0:T(8,128)} %reshape.38), calls=%async_computation | async-start | bytes 1048576 | tf_op jit(solution)/shard_map/all_to_all | solution.py:404
  23.8 0.1 pad_add_fusion.info_ref
  23.9 16.3 %all-to-all-done = f32[128,6,128]{2,1,0:T(8,128)S(1)} async-done(((f32[128,6,128]{2,1,0:T(8,128)}), f32[128,6,128]{2,1,0:T(8,128)S(1)}, u32[]{:S(2)}, u32[]{:S(2)}) %all-to-all-start) | async-done | bytes 393248 | tf_op jit(solution)/shard_map/all_to_all | solution.py:404
  40.2 1.6 %shard_map.86 = (f32[512,128]{1,0:T(8,128)S(1)}, f32[32,32,128]{2,1,0:T(8,128)S(1)}, f32[768,128]{1,0:T(8,128)S(1)}) custom-call(s32[3]{0:T(128)S(1)} %pad_add_fusion.info_ref, f32[768,128]{1,0:T(8,128)S(1)} %reshape.39.got_ref), custom_call_target="tpu_custom_call" | custom-call | flops 1000000 | bytes 1000000 | tf_op jit(solution)/shard_map/pallas_call | solution.py:421
  41.8 3.4 %collective-permute-start = (f32[512,128]{1,0:T(8,128)S(1)}, f32[512,128]{1,0:T(8,128)S(1)}, u32[]{:S(2)}, u32[]{:S(2)}) collective-permute-start(f32[512,128]{1,0:T(8,128)S(1)} %get-tuple-element.9.coeffs_ref), channel_id=1, source_target_pairs={{0,1},{1,0},{2,3},{3,2},{4,5},{5,4},{6,7},{7,6},{8,9},{9,8},{10,11... | collective-permute-start | bytes 786440 | tf_op jit(solution)/shard_map/ppermute | solution.py:426
  45.3 1.2 collective-permute-done.partner_ref
  46.4 18.4 %shard_map.87 = f32[1152,128]{1,0:T(8,128)S(1)} custom-call(s32[3]{0:T(128)S(1)} %pad_add_fusion.info_ref, f32[512,128]{1,0:T(8,128)S(1)} %get-tuple-element.9.coeffs_ref, f32[512,128]{1,0:T(8,128)S(1)} %collective-permute-done.partner_ref, f32[32,32,128]{2,1,0:T(8,128)S(1)} %get-tuple-element.10.leaf_ref, f32[768,128]{1,0:T(8,128)S(1)} %get-tuple-element.11.points_ref), custom_call_target="tpu_custom_call" | custom-call | flops 1000000 | bytes 1000000 | tf_op jit(solution)/shard_map/pallas_call | solution.py:430
  64.8 0.1 reshape.40
  64.9 33.8 %all_to_all.15 = f32[128,9,128]{2,1,0:T(8,128)S(1)} all-to-all(f32[128,9,128]{2,1,0:T(8,128)S(1)} %reshape.40), channel_id=1, replica_groups=mesh['box_0'=4,'box_1'=8,'box_2'=4,'box_3'=2] {'box_0','box_1','box_2'}, dimensions={0} | all-to-all | bytes 1179648 | tf_op jit(solution)/shard_map/all_to_all | solution.py:404
  98.7 0.1 reshape.41.got_ref
  98.8 0.0 copy-start.1
  98.8 0.1 shard_map.88.mine_ref
  98.9 3.5 %collective-permute-start.1 = (f32[8,128]{1,0:T(8,128)S(1)}, f32[8,128]{1,0:T(8,128)S(1)}, u32[]{:S(2)}, u32[]{:S(2)}) collective-permute-start(f32[8,128]{1,0:T(8,128)S(1)} %shard_map.88.mine_ref), channel_id=1, source_target_pairs={{0,1},{1,0},{2,3},{3,2},{4,5},{5,4},{6,7},{7,6},{8,9},{9,8},{10,11... | collective-permute-start | bytes 12296 | tf_op jit(solution)/shard_map/ppermute | solution.py:449
  102.5 0.8 collective-permute-done.1.theirs_ref
  103.3 1.7 %shard_map.89 = (f32[16,4096]{1,0:T(8,128)}, f32[256,128]{1,0:T(8,128)S(1)}, f32[2,16]{1,0:T(2,128)}) custom-call(f32[1152,128]{1,0:T(8,128)S(1)} %reshape.41.got_ref, f32[8,128]{1,0:T(8,128)S(1)} %shard_map.88.mine_ref, f32[8,128]{1,0:T(8,128)S(1)} %collective-permute-done.1.theirs_ref, f32[16,4096]{1,0:T(8,128)S(1)} %copy-done.1), custom_call_target="tpu_custom_call" | custom-call | flops 1000000 | bytes 1000000 | tf_op jit(solution)/shard_map/pallas_call | solution.py:450
  105.0 17.8 %all_to_all.16 = f32[128,2,128]{2,1,0:T(2,128)S(1)} all-to-all(f32[128,2,128]{2,1,0:T(2,128)S(1)} %bitcast.10), channel_id=1, replica_groups=mesh['box_0'=4,'box_1'=8,'box_2'=4,'box_3'=2] {'box_0','box_1','box_2'}, dimensions={0} | all-to-all | bytes 262144 | tf_op jit(solution)/shard_map/all_to_all | solution.py:404
  122.7 0.8 shard_map.90
  (7 shorter events, 0.1 us)
Async XLA Ops:
  0.6 1.0 copy-start
  1.6 0.8 copy-start.2
  2.3 0.7 copy-start.3
  3.1 0.7 copy-start.4
  3.8 0.7 copy-start.5
  6.8 33.4 %all-to-all-start = ((f32[128,6,128]{2,1,0:T(8,128)}), f32[128,6,128]{2,1,0:T(8,128)S(1)}, u32[]{:S(2)}, u32[]{:S(2)}) async-start(f32[128,6,128]{2,1,0:T(8,128)} %reshape.38), calls=%async_computation | async-start | bytes 1048576 | tf_op jit(solution)/shard_map/all_to_all | solution.py:404
  41.8 4.6 %collective-permute-start = (f32[512,128]{1,0:T(8,128)S(1)}, f32[512,128]{1,0:T(8,128)S(1)}, u32[]{:S(2)}, u32[]{:S(2)}) collective-permute-start(f32[512,128]{1,0:T(8,128)S(1)} %get-tuple-element.9.coeffs_ref), channel_id=1, source_target_pairs={{0,1},{1,0},{2,3},{3,2},{4,5},{5,4},{6,7},{7,6},{8,9},{9,8},{10,11... | collective-permute-start | bytes 786440 | tf_op jit(solution)/shard_map/ppermute | solution.py:426
  98.8 4.5 %copy-start.1 = (f32[16,4096]{1,0:T(8,128)S(1)}, f32[16,4096]{1,0:T(8,128)}, u32[]{:S(2)}) copy-start(f32[16,4096]{1,0:T(8,128)} %v_ref.3) | copy-start | bytes 786436
  98.9 4.4 %collective-permute-start.1 = (f32[8,128]{1,0:T(8,128)S(1)}, f32[8,128]{1,0:T(8,128)S(1)}, u32[]{:S(2)}, u32[]{:S(2)}) collective-permute-start(f32[8,128]{1,0:T(8,128)S(1)} %shard_map.88.mine_ref), channel_id=1, source_target_pairs={{0,1},{1,0},{2,3},{3,2},{4,5},{5,4},{6,7},{7,6},{8,9},{9,8},{10,11... | collective-permute-start | bytes 12296 | tf_op jit(solution)/shard_map/ppermute | solution.py:449

commit v2 on v1

v2 whole, which is shorter than its diff:
```python
import functools
import math

import jax
import jax.numpy as jnp
from jax import lax
from jax.experimental import pallas as pl
from jax.experimental.pallas import tpu as pltpu
from jax.sharding import Mesh
from jax.sharding import PartitionSpec as P

RANK = 16
WIDTH = 32
LEAF = 32
SKETCH = 2048
NRHS = 16
SECTIONS = 8
CHIPS = 128
NPTS = 1048576
MOD = 8191
EPS = 1e-06
CHIP = ("box_0", "box_1", "box_2")
CORE = "box_3"
OUT_ROWS = 6
BACK_ROWS = 9
EARLY_MIB = 24
CORE_MIB = 47
F32 = jnp.float32


def fold(x):
    return (x & MOD) + (x >> 13)


def unit_circle(phase):
    r = phase.astype(F32)
    r = jnp.where(r > 4095.5, r - float(MOD), r)
    y = r * (math.pi / MOD)
    y2 = y * y
    s = 1.0 / math.factorial(13)
    for k in (11, 9, 7, 5, 3, 1):
        s = s * y2 + (-1.0) ** (k // 2) / math.factorial(k)
    s = s * y
    c = -1.0 / math.factorial(14)
    for k in (12, 10, 8, 6, 4, 2, 0):
        c = c * y2 + (-1.0) ** (k // 2) / math.factorial(k)
    return 1.0 - 2.0 * s * s, 2.0 * s * c


def times(a, b):
    return a[0] * b[0] - a[1] * b[1], a[0] * b[1] + a[1] * b[0]


def split_rows(lhs, y, high, cols):
    top = y.astype(jnp.bfloat16).astype(F32)
    for p, part in enumerate((top, y - top)):
        for h in range(8):
            mask = jnp.broadcast_to(high == h, (NRHS, 128))
            lhs[pl.ds(p * 128 + h * 16, 16), cols] = jnp.where(mask, part, 0.0).astype(jnp.bfloat16)


def hot_rows(rhs, low, cols):
    index = lax.broadcasted_iota(jnp.int32, (256, 128), 0)
    rhs[:, cols] = jnp.where(index == low, 1.0, 0.0).astype(jnp.bfloat16)


def sketched(lhs, rhs, out_ref, at, stride):
    both = lax.dot_general(
        lhs[...], rhs[...], (((1,), (1,)), ((), ())), preferred_element_type=F32
    )
    both = both[0:128] + both[128:256]
    for half in range(2):
        tile = jnp.concatenate(
            [
                both[(t // 2) * 16 : (t // 2) * 16 + 16, (t % 2) * 128 : (t % 2) * 128 + 128]
                for t in range(half * 8, half * 8 + 8)
            ],
            0,
        )
        out_ref[pl.ds(at + half, 128, stride=stride), :] = tile.T


def fetch(sources, held, sems):
    copies = [pltpu.make_async_copy(a, b, sems.at[i]) for i, (a, b) in enumerate(zip(sources, held))]
    for copy in copies:
        copy.start()
    for copy in copies:
        copy.wait()


def pack_kernel(*refs):
    sources, out_ref, held, turned, sems = refs[:5], refs[5], refs[6:11], refs[11], refs[12]
    fetch(sources, held, sems)
    v_ref, coords_ref, diag_ref, rows_ref, signs_ref = held
    zeros = jnp.zeros((11, 128), F32)
    for jb in range(8):
        tiles = []
        for jt in range(4):
            j = jb * 4 + jt
            cols = pl.ds(j * 128, 128)
            tiles += [
                v_ref[:, cols],
                coords_ref[:, cols].astype(F32),
                diag_ref[j : j + 1, :],
                rows_ref[j : j + 1, :].astype(F32),
                signs_ref[j : j + 1, :].astype(F32),
                zeros,
            ]
        turned[pl.ds(jb * 128, 128), :] = jnp.concatenate(tiles, 0).T
    lane = lax.broadcasted_iota(jnp.int32, (32, 128), 1)
    for jt in range(4):
        made = {}
        for s in range(LEAF):
            rows = turned[pl.ds(s, 32, stride=32), :]
            for col, start, at in (
                (s // 8, jt * 32, 16 * (s % 8)),
                (4 + s // 16, jt * 32 + 16, 8 * (s % 16)),
            ):
                shift = (at - start) % 128
                moved = pltpu.roll(rows, shift, 1) if shift else rows
                if col in made:
                    moved = jnp.where(lane >= at, moved, made[col])
                made[col] = moved
        for col, rows in made.items():
            out_ref[pl.ds(jt * 32 * OUT_ROWS + col, 32, stride=OUT_ROWS), :] = rows


def product(out_count, terms, store, start=None, width=16, group=8):
    def tile(t, carry):
        accs = [jnp.zeros((8, 128), F32)] * (2 * width)
        if start is not None:
            accs = [x for i in range(width) for x in start(t * width + i)]

        def some(g, accs):
            accs = list(accs)
            for matrix, vector in terms:
                for i in range(group):
                    b = g * group + i
                    vec = vector(b)
                    for i in range(width):
                        row = jnp.broadcast_to(matrix(t * width + i, b), (8, 128))
                        for half in range(2):
                            accs[2 * i + half] += row * vec[half]
            return tuple(accs)

        accs = lax.fori_loop(0, 32 // group, some, tuple(accs))
        for i in range(width):
            store(t * width + i, accs[2 * i : 2 * i + 2])
        return carry

    lax.fori_loop(0, out_count // width, tile, 0)


def halves(ref, a, *lead):
    return [ref[(*lead, pl.ds(pl.multiple_of(a * 16 + 8 * h, 8), 8), slice(None))] for h in range(2)]


def row16(a):
    return pl.ds(pl.multiple_of(a * 16, 16), 16)


def leaf_kernel(info_ref, got_ref, after_ref, coeffs_ref, leaf_ref, points_ref):
    for c in range(6):
        points_ref[pl.ds(c * 128, 128), :] = got_ref[pl.ds(c, 128, stride=OUT_ROWS), :].T
    scale = info_ref[0]

    def powers(field):
        where = points_ref[pl.ds(512 + field, 32, stride=8), :].astype(jnp.int32)
        one = unit_circle(fold(fold(where * scale)))
        two = times(one, one)
        return [one, two, times(two, one), times(two, two)]

    first, second = powers(0), powers(1)
    gain = 1.0 / math.sqrt(LEAF)
    second = [(c * gain, s * gain) for c, s in second]
    for w in range(RANK):
        c, s = times(first[w % 4], second[w // 4])
        leaf_ref[w] = c
        leaf_ref[w + RANK] = s

    def store(a, x):
        coeffs_ref[row16(a), :] = jnp.concatenate(x, 0)

    product(
        WIDTH,
        [(lambda a, b: leaf_ref[a, pl.ds(b, 1), :], lambda b: halves(points_ref, b))],
        store,
    )


def section_map(map_ref, unit, offset, first_power, turn, gain):
    index = lax.broadcasted_iota(jnp.int32, (WIDTH, 128), 0) + offset
    one = unit_circle(fold(fold(unit * index)))
    two = times(one, one)
    four = times(two, two)
    scale = (gain * math.cos(turn), gain * math.sin(turn))
    power = one if first_power == 1 else times(two, one)
    power = (
        power[0] * scale[0] - power[1] * scale[1],
        power[0] * scale[1] + power[1] * scale[0],
    )
    fine = [power]
    for _ in range(3):
        fine.append(times(fine[-1], one))
    coarse = None
    for i in range(8):
        for j in range(4):
            c, s = fine[j]
            map_ref[4 * i + j] = c if coarse is None else coarse[0] * c - coarse[1] * s
        coarse = four if coarse is None else times(coarse, four)


def state_rows(parts):
    pad = [jnp.zeros((128 - 16 * len(parts), 128), F32)]
    return jnp.sum(jnp.concatenate(parts + pad, 0).T, axis=0, keepdims=True)


def section_maps(info_ref, k, maps_ref):
    scale, chip, core = info_ref[0], info_ref[1], info_ref[2]
    place = ((chip >> 2) & 7) * 16 + (chip >> 5) * 4 + (chip & 3)
    lane = lax.broadcasted_iota(jnp.int32, (1, 128), 1)
    key = ((lane * 2 + core) * 128 + place) * 37 + 101 * k
    whole = (key.astype(F32) * (1.0 / (MOD - 1))).astype(jnp.int32)
    key = key - whole * (MOD - 1)
    key = jnp.where(key < 0, key + (MOD - 1), key)
    key = jnp.where(key >= MOD - 1, key - (MOD - 1), key)
    unit = fold(fold((key + 1) * scale))
    turn = 2.0 * math.pi * 4096 / MOD
    section_map(maps_ref.at[0], unit, 2, 1, 0.0, 0.35 / math.sqrt(WIDTH))
    section_map(maps_ref.at[1], unit, 1, 3, turn, 0.6 / math.sqrt(WIDTH))


def early_kernel(info_ref, *refs):
    sources, maps_ref, sketch_ref, done_ref = refs[:3], *refs[3:6]
    held, lhs, rhs, sems = refs[6:9], *refs[9:]
    fetch(sources, held, sems)
    v_ref, rows_ref, signs_ref = held

    def section(k, carry):
        section_maps(info_ref, k, maps_ref.at[k - 1])
        return carry

    lax.fori_loop(1, SECTIONS, section, 0)
    for j in range(32):
        cols = pl.ds(j * 128, 128)
        rows, signs = rows_ref[j : j + 1, :], signs_ref[j : j + 1, :]
        split_rows(lhs, v_ref[:, cols] * (2 * signs - 1).astype(F32), rows >> 8, cols)
        hot_rows(rhs, rows & 255, cols)
    sketched(lhs, rhs, sketch_ref, 0, 2)
    done_ref[...] = jnp.zeros((8, 128), F32)


def hot_kernel(info_ref, points_ref, rhs_ref, maps_ref):
    for s in range(LEAF):
        low = points_ref[pl.ds(512 + s * 8 + 3, 1), :].astype(jnp.int32) & 255
        hot_rows(rhs_ref, low, pl.ds(s * 128, 128))
    section_maps(info_ref, 0, maps_ref)


def core_kernel(
    coeffs_ref,
    partner_ref,
    leaf_ref,
    points_ref,
    first,
    rhs,
    vsketch_ref,
    maps_hbm,
    out_ref,
    now,
    other,
    image,
    lhs,
    maps,
    sems,
):
    lane = lax.broadcasted_iota(jnp.int32, (1, 128), 1)
    lanes = lax.broadcasted_iota(jnp.int32, (NRHS, 128), 1)

    def copy(k):
        return pltpu.make_async_copy(maps_hbm.at[k - 1], maps.at[k & 1], sems.at[k & 1])

    copy(1).start()
    now[0] = coeffs_ref[...]
    other[0] = partner_ref[...]

    def section(k, own, cross):
        at = k & 1
        step = jnp.left_shift(1, jnp.minimum(k, SECTIONS - 2))
        bit = (lanes & step) == 0

        def store(a, x):
            x = jnp.concatenate(x, 0)
            now[1 - at, row16(a), :] = x
            other[1 - at, row16(a), :] = jnp.where(
                bit, pltpu.roll(x, 128 - step, 1), pltpu.roll(x, step, 1)
            )

        product(
            WIDTH,
            [
                (lambda a, b: own[a, pl.ds(b, 1), :], lambda b: halves(now, b, at)),
                (lambda a, b: cross[a, pl.ds(b, 1), :], lambda b: halves(other, b, at)),
            ],
            store,
            lambda a: [0.85 * x for x in jnp.split(now[at, row16(a), :], 2)],
        )

    section(jnp.int32(0), first.at[0], first.at[1])

    def later(k, carry):
        copy(k).wait()

        @pl.when(k < SECTIONS - 1)
        def _():
            copy(k + 1).start()

        section(k, maps.at[k & 1, 0], maps.at[k & 1, 1])
        return carry

    lax.fori_loop(1, SECTIONS, later, 0)

    square = jnp.zeros((NRHS, 128), F32)
    inner = jnp.zeros((NRHS, 128), F32)
    for t in range(2):
        accs = [None] * 16
        for w in range(WIDTH):
            vec = now[0, pl.ds(w * 16, 16), :]
            for i in range(16):
                s = t * 16 + i
                term = leaf_ref[w, s : s + 1, :] * vec
                accs[i] = term if accs[i] is None else accs[i] + term
        for i in range(16):
            s = t * 16 + i
            v = points_ref[pl.ds(s * 16, 16), :]
            x = points_ref[pl.ds(512 + s * 8 + 2, 1), :] * v + accs[i]
            image[pl.ds(s * 16, 16), :] = x
            square += v * v
            inner += v * x
            sign = 2.0 * points_ref[pl.ds(512 + s * 8 + 4, 1), :] - 1.0
            high = points_ref[pl.ds(512 + s * 8 + 3, 1), :].astype(jnp.int32) >> 8
            split_rows(lhs, x * sign, high, pl.ds(s * 128, 128))
    sums = state_rows([square, inner])
    valid = lane < 16
    vv = jnp.where(valid, sums, 0.0)
    iv = jnp.where(valid, pltpu.roll(sums, 112, 1), 0.0)
    local = jnp.where(vv > 0.0, iv / jnp.where(vv > 0.0, vv, 1.0), 0.0)
    across = jnp.broadcast_to(local, (128, 128)).T[0:NRHS, :]
    energy = jnp.zeros((NRHS, 128), F32)
    mixed = jnp.zeros((NRHS, 128), F32)
    for s in range(LEAF):
        v = points_ref[pl.ds(s * 16, 16), :]
        r = image[pl.ds(s * 16, 16), :] - across * v
        energy += r * r
        mixed += r * v
    for c in range(4):
        out_ref[pl.ds(c, 128, stride=BACK_ROWS), :] = image[pl.ds(c * 128, 128), :].T
    for c in range(2):
        out_ref[pl.ds(6 + c, 128, stride=BACK_ROWS), :] = vsketch_ref[pl.ds(c, 128, stride=2), :]
    sketched(lhs, rhs, out_ref, 4, BACK_ROWS)
    rest = jnp.where(lane < 32, state_rows([energy, mixed]), 0.0)
    state = vv + pltpu.roll(local, 16, 1) + pltpu.roll(rest, 32, 1)
    out_ref[pl.ds(8, 128, stride=BACK_ROWS), :] = jnp.broadcast_to(state, (128, 128))


def merged(vv, p, e, cr, total):
    square = total(vv)
    inner = total(p * vv + cr)
    local = jnp.where(square > 0.0, inner / jnp.where(square > 0.0, square, 1.0), 0.0)
    return square, inner, local


def moved_energy(vv, p, e, cr, at, total):
    off = p - at
    return total(e + off * (2.0 * cr + off * vv)), total(cr + off * vv)


def sum_kernel(got_ref, out_ref):
    for c in range(4):
        out_ref[c : c + 1, :] = jnp.sum(
            got_ref[pl.ds(4 + c, 128, stride=BACK_ROWS), :], axis=0, keepdims=True
        )
    state = got_ref[pl.ds(8, 128, stride=BACK_ROWS), :]
    valid = lax.broadcasted_iota(jnp.int32, (128, 128), 1) < 16
    parts = [
        jnp.where(valid, pltpu.roll(state, (128 - 16 * i) % 128, 1) if i else state, 0.0)
        for i in range(4)
    ]

    def total(x):
        return jnp.sum(x, axis=0, keepdims=True)

    square, inner, local = merged(*parts, total)
    energy, mixed = moved_energy(*parts, local, total)
    for i, x in enumerate((square, local, energy, mixed)):
        out_ref[4 + i : 5 + i, :] = x


def chunk_kernel(mine_ref, theirs_ref, chunk_ref, arnoldi_ref, scalars_ref):
    both = [(mine_ref[4 + i : 5 + i, :], theirs_ref[4 + i : 5 + i, :]) for i in range(4)]
    vv, p, e, cr = both
    square = vv[0] + vv[1]
    inner = (p[0] * vv[0] + cr[0]) + (p[1] * vv[1] + cr[1])
    proj = (inner / NPTS) / (square / NPTS + EPS)
    terms = []
    for i in range(2):
        off = p[i] - proj
        terms.append(e[i] + off * (2.0 * cr[i] + off * vv[i]))
    spread = jnp.sqrt(jnp.maximum(terms[0] + terms[1], 0.0) / NPTS + EPS)
    arnoldi_ref[0:1, :] = proj[:, 0:NRHS]
    arnoldi_ref[1:2, :] = spread[:, 0:NRHS]
    valid = lax.broadcasted_iota(jnp.int32, (1, 128), 1) < 16

    def tiled(x):
        x = jnp.where(valid, x, 0.0)
        for shift in (16, 32, 64):
            x = x + pltpu.roll(x, shift, 1)
        return x

    proj, spread = tiled(proj), tiled(spread)
    scalars_ref[0:1, :] = proj
    scalars_ref[1:2, :] = spread
    sums = mine_ref[0:4, :] + theirs_ref[0:4, :]
    chunk = (sums[0:2] - proj * sums[2:4]) / spread * math.sqrt(SKETCH / NPTS)
    for i in range(2):
        chunk_ref[pl.ds(i, 128, stride=2), :] = jnp.broadcast_to(chunk[i : i + 1], (128, 128))


def basis_kernel(got_ref, scalars_ref, v_ref, basis_ref, turned):
    proj = jnp.broadcast_to(scalars_ref[0:1, :], (128, 128)).T[0:NRHS, :]
    spread = jnp.broadcast_to(scalars_ref[1:2, :], (128, 128)).T[0:NRHS, :]
    lane = lax.broadcasted_iota(jnp.int32, (32, 128), 1)
    for s in range(LEAF):
        made = None
        for jt in range(4):
            rows = got_ref[pl.ds(jt * 32 * BACK_ROWS + s // 8, 32, stride=BACK_ROWS), :]
            shift = (jt * 32 - (s % 8) * 16) % 128
            rows = pltpu.roll(rows, shift, 1) if shift else rows
            made = rows if made is None else jnp.where(lane >= jt * 32, rows, made)
        turned[pl.ds(s, 32, stride=32), :] = made
    for jb in range(8):
        back = turned[pl.ds(jb * 128, 128), :].T
        for jt in range(4):
            cols = pl.ds((jb * 4 + jt) * 128, 128)
            x = back[jt * 32 : jt * 32 + 16, :]
            basis_ref[:, cols] = (x - proj * v_ref[:, cols]) / spread


def spread_kernel(got_ref, out_ref):
    for half in range(2):
        tile = got_ref[pl.ds(half, 128, stride=2), :].T
        for t in range(8):
            out_ref[:, pl.ds((half * 8 + t) * 128, 128)] = tile[t * 16 : t * 16 + 16, :]


VMEM = pl.BlockSpec(memory_space=pltpu.VMEM)
SMEM = pl.BlockSpec(memory_space=pltpu.SMEM)
HBM = pl.BlockSpec(memory_space=pltpu.HBM)


def f32(*shape):
    return jax.ShapeDtypeStruct(shape, F32)


def call(kernel, out, ins, scratch=(), flops=1000000, mib=12):
    single = not isinstance(out, tuple)
    return pl.pallas_call(
        kernel,
        out_shape=out,
        in_specs=ins,
        out_specs=VMEM if single else tuple(VMEM for _ in out),
        scratch_shapes=list(scratch),
        cost_estimate=pl.CostEstimate(flops=flops, bytes_accessed=1000000, transcendentals=0),
        compiler_params=pltpu.CompilerParams(vmem_limit_bytes=mib * 1024 * 1024),
    )


def exchange(x):
    return lax.all_to_all(x[:, None, :], CHIP, 0, 0, tiled=True)[:, 0, :]


def body(basis_vector, diagonal, coords, phase_scale, sketch_rows, sketch_signs):
    chip = lax.axis_index(CHIP)
    core = lax.axis_index(CORE)
    info = jnp.stack([phase_scale[0] % MOD, chip, core]).astype(jnp.int32)
    points = LEAF * CHIPS
    swap = [(0, 1), (1, 0)]
    sketch_rows, sketch_signs = sketch_rows.reshape(32, 128), sketch_signs.reshape(32, 128)
    vector = pltpu.VMEM((NRHS, points), F32)
    ints = pltpu.VMEM((32, 128), jnp.int32)
    turned = pltpu.VMEM((1024, 128), F32)
    parts = pltpu.VMEM((256, points), jnp.bfloat16)
    hot_type = jax.ShapeDtypeStruct((256, points), jnp.bfloat16)
    packed = call(
        pack_kernel,
        f32(CHIPS * OUT_ROWS, 128),
        [HBM] * 5,
        [
            vector,
            pltpu.VMEM((2, points), jnp.int32),
            pltpu.VMEM((32, 128), F32),
            ints,
            ints,
            turned,
            pltpu.SemaphoreType.DMA((5,)),
        ],
        mib=60,
    )(basis_vector, coords, diagonal.reshape(32, 128), sketch_rows, sketch_signs)
    maps, vsketch, done = call(
        early_kernel,
        (f32(SECTIONS - 1, 2, WIDTH, WIDTH, 128), f32(CHIPS * 2, 128), f32(8, 128)),
        [SMEM] + [HBM] * 3,
        [vector, ints, ints, parts, parts, pltpu.SemaphoreType.DMA((3,))],
        flops=20000000,
        mib=EARLY_MIB,
    )(info, basis_vector, sketch_rows, sketch_signs)
    got = exchange(packed)
    coeffs, leaf, held = call(
        leaf_kernel,
        (f32(512, 128), f32(WIDTH, LEAF, 128), f32(OUT_ROWS * 128, 128)),
        [SMEM, VMEM, HBM],
    )(info, got, done)
    partner = lax.ppermute(coeffs, CORE, swap)
    first_type = f32(2, WIDTH, WIDTH, 128)
    hot, first = call(hot_kernel, (hot_type, first_type), [SMEM, VMEM])(info, held)
    pair = pltpu.VMEM((2, 512, 128), F32)
    back = call(
        core_kernel,
        f32(CHIPS * BACK_ROWS, 128),
        [VMEM] * 7 + [HBM],
        [
            pair,
            pair,
            pltpu.VMEM((512, 128), F32),
            parts,
            pltpu.VMEM((2, 2, WIDTH, WIDTH, 128), F32),
            pltpu.SemaphoreType.DMA((2,)),
        ],
        mib=CORE_MIB,
    )(coeffs, partner, leaf, held, first, hot, vsketch, maps)
    home = exchange(back)
    mine = call(sum_kernel, f32(8, 128), [VMEM])(home)
    theirs = lax.ppermute(mine, CORE, swap)
    chunk, arnoldi, scalars = call(
        chunk_kernel, (f32(CHIPS * 2, 128), f32(2, NRHS), f32(2, 128)), [VMEM] * 2
    )(mine, theirs)
    spread = exchange(chunk)
    new_basis = call(basis_kernel, f32(NRHS, points), [VMEM] * 3, [turned], flops=20000000)(
        home, scalars, basis_vector
    )
    sketch = call(spread_kernel, f32(NRHS, SKETCH), [VMEM])(spread)
    return new_basis, sketch, arnoldi


def solution(mesh):
    torus = Mesh(mesh.devices.reshape(4, 8, 4, 2), ("box_0", "box_1", "box_2", "box_3"))
    box = ("box_0", "box_1", "box_2", "box_3")
    placed = (P(None, box), P(box), P(None, box), P(), P(box), P(box))
    return jax.shard_map(
        body, mesh=torus, in_specs=placed, out_specs=(P(None, box), P(), P()), check_vma=False
    )
```

time: 124 us -> 104 us (0.84)
  blocking collectives: 51.6 us -> 25.3 us
  starting transfers between devices: 23.3 us -> 29.2 us
  waiting for transfers between devices: 18.3 us -> 14.7 us
  Pallas kernels: 24 us -> 27.4 us
    all_to_all x2 -> x1, blocking collectives: 51.6 us -> 25.3 us  [exchange(): return lax.all_to_all(x[:, None, :], CHIP, 0, 0, tiled=True)[:, 0, :]]
    all_to_all x1 -> x2, starting transfers between devices: 16.3 us -> 23.6 us  [exchange(): return lax.all_to_all(x[:, None, :], CHIP, 0, 0, tiled=True)[:, 0, :]]
    pallas_call x5 -> x8, Pallas kernels: 23.8 us -> 27.2 us  [the longest x1 13.6 us: body(): call(core_kernel, f32(CHIPS * BACK_ROWS, 128), [VMEM] * 7 + [HBM], [pair,...]
    all_to_all x1 -> x2, waiting for transfers between devices: 16.3 us -> 13.9 us  [exchange(): return lax.all_to_all(x[:, None, :], CHIP, 0, 0, tiled=True)[:, 0, :]]
    unnamed x12 -> x10, local copies, waits for them, and re-layouts: 3.86 us -> 5.33 us
    ppermute x2, starting transfers between devices: 6.97 us -> 5.64 us  [the longest x1 3.1 us: body(): partner = lax.ppermute(coeffs, CORE, swap)]
  transfers between devices with their start and end apart: 3 -> 4, of which waited for: 3 -> 3; matrix products, arithmetic and copies ran while one was open for 0% -> 0% of each run, Pallas kernels for 0% -> 7%
where the time goes in v2:
time: 104 us; the launch traced here: 103 us
  starting transfers between devices  29.2 us (28%)
  Pallas kernels  27.4 us (26%)
  blocking collectives  25.3 us (24%)
  waiting for transfers between devices  14.7 us (14%)
  local copies, waits for them, and re-layouts  5.33 us (5%)
  between operations  1.4 us (1%)
    all_to_all x1, blocking collectives, exchange(): return lax.all_to_all(x[:, None, :], CHIP, 0, 0, tiled=True)[:, 0, :]  25.3 us
    all_to_all x2, starting transfers between devices, exchange(): return lax.all_to_all(x[:, None, :], CHIP, 0, 0, tiled=True)[:, 0, :]  23.6 us
    all_to_all x2, waiting for transfers between devices, exchange(): return lax.all_to_all(x[:, None, :], CHIP, 0, 0, tiled=True)[:, 0, :]  13.9 us
    pallas_call x1, Pallas kernels, body(): call(core_kernel, f32(CHIPS * BACK_ROWS, 128), [VMEM] * 7 + [HBM], [pair,...  13.6 us
    unnamed x10, local copies, waits for them, and re-layouts  5.33 us
    pallas_call x1, Pallas kernels, body(): call(early_kernel, (f32(SECTIONS - 1, 2, WIDTH, WIDTH, 128), f32(CHIPS *...  4.27 us
    pallas_call x1, Pallas kernels, body(): call(pack_kernel, f32(CHIPS * OUT_ROWS, 128), [HBM] * 5, [vector, pltpu.V...  3.22 us
    ppermute x1, starting transfers between devices, body(): partner = lax.ppermute(coeffs, CORE, swap)  3.1 us
  transfers between devices with their start and end apart: 4, of which 3 were waited for; matrix products, arithmetic and copies ran while one was open for 0% of the time, Pallas kernels for 7%

profile of v2, /device:TPU:1, one launch (start us, length us, event | category | flops | bytes accessed | tf_op | source)
XLA Modules:
  0.0 103.4 jit_solution(9610634107059455199)
XLA Ops:
  0.6 3.2 %shard_map.85 = f32[768,128]{1,0:T(8,128)} custom-call(f32[16,4096]{1,0:T(8,128)} %v_ref.1, s32[2,4096]{1,0:T(2,128)} %refs_1_.1, f32[32,128]{1,0:T(8,128)} %bitcast.29, s32[32,128]{1,0:T(8,128)} %bitcast.24, s32[32,128]{1,0:T(8,128)} %bitcast.26), custom_call_target="tpu_custom_call" | custom-call | flops 1000000 | bytes 1000000 | tf_op jit(solution)/shard_map/pallas_call | solution.py:494
  3.9 16.3 %all-to-all-start = ((f32[768,1,128]{2,1,0:T(1,128)}), f32[768,1,128]{2,1,0:T(1,128)S(1)}, u32[]{:S(2)}, u32[]{:S(2)}) async-start(f32[768,1,128]{2,1,0:T(1,128)} %bitcast.28), calls=%async_computation | async-start | bytes 786432 | tf_op jit(solution)/shard_map/all_to_all | solution.py:479
  20.9 0.1 pad_add_fusion.info_ref
  21.0 0.9 copy-done.1
  21.9 0.7 copy-done.3
  22.6 0.7 copy-done.4
  23.3 4.3 %shard_map.86 = (f32[7,2,32,32,128]{4,3,2,1,0:T(8,128)S(1)}, f32[256,128]{1,0:T(8,128)S(1)}, f32[8,128]{1,0:T(8,128)S(1)}) custom-call(s32[3]{0:T(128)S(1)} %pad_add_fusion.info_ref, f32[16,4096]{1,0:T(8,128)S(1)} %copy-done.1, s32[32,128]{1,0:T(8,128)S(1)} %bitcast.25, s32[32,128]{1,0:T(8,128)S(1)} %bitcast.27), custom_call_target="tpu_custom_call" | custom-call | flops 20000000 | bytes 1000000 | tf_op jit(solution)/shard_map/pallas_call | solution.py:509
  27.6 2.9 %copy-done = f32[7,2,32,32,128]{4,3,2,1,0:T(8,128)} copy-done((f32[7,2,32,32,128]{4,3,2,1,0:T(8,128)}, f32[7,2,32,32,128]{4,3,2,1,0:T(8,128)S(1)}, u32[]{:S(2)}) %copy-start) | copy-done | bytes 7340056
  30.6 4.6 %all-to-all-done = f32[768,1,128]{2,1,0:T(1,128)S(1)} async-done(((f32[768,1,128]{2,1,0:T(1,128)}), f32[768,1,128]{2,1,0:T(1,128)S(1)}, u32[]{:S(2)}, u32[]{:S(2)}) %all-to-all-start) | async-done | bytes 393248 | tf_op jit(solution)/shard_map/all_to_all | solution.py:479
  35.2 1.5 %shard_map.87 = (f32[512,128]{1,0:T(8,128)S(1)}, f32[32,32,128]{2,1,0:T(8,128)S(1)}, f32[768,128]{1,0:T(8,128)S(1)}) custom-call(s32[3]{0:T(128)S(1)} %pad_add_fusion.info_ref, f32[768,128]{1,0:T(8,128)S(1)} %bitcast.22, f32[8,128]{1,0:T(8,128)S(1)} %get-tuple-element.14.after_ref), custom_call_target="tpu_custom_call" | custom-call | flops 1000000 | bytes 1000000 | tf_op jit(solution)/shard_map/pallas_call | solution.py:518
  36.7 3.1 %collective-permute-start = (f32[512,128]{1,0:T(8,128)S(1)}, f32[512,128]{1,0:T(8,128)S(1)}, u32[]{:S(2)}, u32[]{:S(2)}) collective-permute-start(f32[512,128]{1,0:T(8,128)S(1)} %get-tuple-element.15.coeffs_ref), channel_id=1, source_target_pairs={{0,1},{1,0},{2,3},{3,2},{4,5},{5,4},{6,7},{7,6},{8,9},{9,8},{10,11... | collective-permute-start | bytes 786440 | tf_op jit(solution)/shard_map/ppermute | solution.py:523
  39.8 1.3 %shard_map.88 = (bf16[256,4096]{1,0:T(8,128)(2,1)S(1)}, f32[2,32,32,128]{3,2,1,0:T(8,128)S(1)}) custom-call(s32[3]{0:T(128)S(1)} %pad_add_fusion.info_ref, f32[768,128]{1,0:T(8,128)S(1)} %get-tuple-element.17.points_ref), custom_call_target="tpu_custom_call" | custom-call | flops 1000000 | bytes 1000000 | tf_op jit(solution)/shard_map/pallas_call | solution.py:525
  41.1 0.0 collective-permute-done.partner_ref
  41.1 0.0 copy-start.2
  41.1 13.6 %shard_map.89 = f32[1152,128]{1,0:T(8,128)S(1)} custom-call(f32[512,128]{1,0:T(8,128)S(1)} %get-tuple-element.15.coeffs_ref, f32[512,128]{1,0:T(8,128)S(1)} %collective-permute-done.partner_ref, f32[32,32,128]{2,1,0:T(8,128)S(1)} %get-tuple-element.16.leaf_ref, f32[768,128]{1,0:T(8,128)S(1)} %get-tuple-element.17.points_ref, ...), custom_call_target="tpu_custom_call" | custom-call | flops 1000000 | bytes 1000000 | tf_op jit(solution)/shard_map/pallas_call | solution.py:527
  54.7 25.3 %all_to_all.15 = f32[1152,1,128]{2,1,0:T(1,128)S(1)} all-to-all(f32[1152,1,128]{2,1,0:T(1,128)S(1)} %bitcast.21), channel_id=1, replica_groups=mesh['box_0'=4,'box_1'=8,'box_2'=4,'box_3'=2] {'box_0','box_1','box_2'}, dimensions={0} | all-to-all | bytes 1179648 | tf_op jit(solution)/shard_map/all_to_all | solution.py:479
  80.0 0.1 shard_map.90.mine_ref
  80.2 2.5 %collective-permute-start.1 = (f32[8,128]{1,0:T(8,128)S(1)}, f32[8,128]{1,0:T(8,128)S(1)}, u32[]{:S(2)}, u32[]{:S(2)}) collective-permute-start(f32[8,128]{1,0:T(8,128)S(1)} %shard_map.90.mine_ref), channel_id=1, source_target_pairs={{0,1},{1,0},{2,3},{3,2},{4,5},{5,4},{6,7},{7,6},{8,9},{9,8},{10,11... | collective-permute-start | bytes 12296 | tf_op jit(solution)/shard_map/ppermute | solution.py:543
  82.7 0.8 collective-permute-done.1.theirs_ref
  83.5 0.9 shard_map.91
  84.4 7.3 %all-to-all-start.2 = ((f32[256,1,128]{2,1,0:T(1,128)}), f32[256,1,128]{2,1,0:T(1,128)S(1)}, u32[]{:S(2)}, u32[]{:S(2)}) async-start(f32[256,1,128]{2,1,0:T(1,128)} %bitcast.14), calls=%async_computation.2 | async-start | bytes 262144 | tf_op jit(solution)/shard_map/all_to_all | solution.py:479
  91.7 1.6 %shard_map.92 = f32[16,4096]{1,0:T(8,128)} custom-call(f32[1152,128]{1,0:T(8,128)S(1)} %bitcast.20, f32[2,128]{1,0:T(2,128)S(1)} %get-tuple-element.22.scalars_ref, f32[16,4096]{1,0:T(8,128)S(1)} %copy-done.2), custom_call_target="tpu_custom_call" | custom-call | flops 20000000 | bytes 1000000 | tf_op jit(solution)/shard_map/pallas_call | solution.py:548
  93.4 9.3 %all-to-all-done.2 = f32[256,1,128]{2,1,0:T(1,128)S(1)} async-done(((f32[256,1,128]{2,1,0:T(1,128)}), f32[256,1,128]{2,1,0:T(1,128)S(1)}, u32[]{:S(2)}, u32[]{:S(2)}) %all-to-all-start.2) | async-done | bytes 131104 | tf_op jit(solution)/shard_map/all_to_all | solution.py:479
  102.6 0.8 shard_map.93
  (5 shorter events, 0.0 us)
Async XLA Ops:
  3.9 31.3 %all-to-all-start = ((f32[768,1,128]{2,1,0:T(1,128)}), f32[768,1,128]{2,1,0:T(1,128)S(1)}, u32[]{:S(2)}, u32[]{:S(2)}) async-start(f32[768,1,128]{2,1,0:T(1,128)} %bitcast.28), calls=%async_computation | async-start | bytes 786432 | tf_op jit(solution)/shard_map/all_to_all | solution.py:479
  21.0 1.0 copy-start.1
  21.9 0.7 copy-start.3
  22.6 0.7 copy-start.4
  27.6 2.9 %copy-start = (f32[7,2,32,32,128]{4,3,2,1,0:T(8,128)}, f32[7,2,32,32,128]{4,3,2,1,0:T(8,128)S(1)}, u32[]{:S(2)}) copy-start(f32[7,2,32,32,128]{4,3,2,1,0:T(8,128)S(1)} %get-tuple-element.21.maps_hbm) | copy-start | bytes 22020100
  36.7 4.4 %collective-permute-start = (f32[512,128]{1,0:T(8,128)S(1)}, f32[512,128]{1,0:T(8,128)S(1)}, u32[]{:S(2)}, u32[]{:S(2)}) collective-permute-start(f32[512,128]{1,0:T(8,128)S(1)} %get-tuple-element.15.coeffs_ref), channel_id=1, source_target_pairs={{0,1},{1,0},{2,3},{3,2},{4,5},{5,4},{6,7},{7,6},{8,9},{9,8},{10,11... | collective-permute-start | bytes 786440 | tf_op jit(solution)/shard_map/ppermute | solution.py:523
  41.1 50.6 %copy-start.2 = (f32[16,4096]{1,0:T(8,128)S(1)}, f32[16,4096]{1,0:T(8,128)}, u32[]{:S(2)}) copy-start(f32[16,4096]{1,0:T(8,128)} %v_ref.1) | copy-start | bytes 786436
  80.2 3.4 %collective-permute-start.1 = (f32[8,128]{1,0:T(8,128)S(1)}, f32[8,128]{1,0:T(8,128)S(1)}, u32[]{:S(2)}, u32[]{:S(2)}) collective-permute-start(f32[8,128]{1,0:T(8,128)S(1)} %shard_map.90.mine_ref), channel_id=1, source_target_pairs={{0,1},{1,0},{2,3},{3,2},{4,5},{5,4},{6,7},{7,6},{8,9},{9,8},{10,11... | collective-permute-start | bytes 12296 | tf_op jit(solution)/shard_map/ppermute | solution.py:543
  84.4 18.2 %all-to-all-start.2 = ((f32[256,1,128]{2,1,0:T(1,128)}), f32[256,1,128]{2,1,0:T(1,128)S(1)}, u32[]{:S(2)}, u32[]{:S(2)}) async-start(f32[256,1,128]{2,1,0:T(1,128)} %bitcast.14), calls=%async_computation.2 | async-start | bytes 262144 | tf_op jit(solution)/shard_map/all_to_all | solution.py:479

commit v3 on v2

--- a/solution.py
+++ b/solution.py
@@ -22,8 +22,9 @@
 CHIP = ("box_0", "box_1", "box_2")
 CORE = "box_3"
 OUT_ROWS = 6
-BACK_ROWS = 9
-EARLY_MIB = 24
+SUM_ROWS = 4
+BACK_ROWS = 6
+EARLY_MIB = 48
 CORE_MIB = 47
 F32 = jnp.float32
 
@@ -64,33 +65,34 @@
     rhs[:, cols] = jnp.where(index == low, 1.0, 0.0).astype(jnp.bfloat16)
 
 
-def sketched(lhs, rhs, out_ref, at, stride):
+def sketched(lhs, rhs):
     both = lax.dot_general(
         lhs[...], rhs[...], (((1,), (1,)), ((), ())), preferred_element_type=F32
     )
     both = both[0:128] + both[128:256]
-    for half in range(2):
-        tile = jnp.concatenate(
+    return [
+        jnp.concatenate(
             [
                 both[(t // 2) * 16 : (t // 2) * 16 + 16, (t % 2) * 128 : (t % 2) * 128 + 128]
                 for t in range(half * 8, half * 8 + 8)
             ],
             0,
-        )
-        out_ref[pl.ds(at + half, 128, stride=stride), :] = tile.T
-
-
-def fetch(sources, held, sems):
-    copies = [pltpu.make_async_copy(a, b, sems.at[i]) for i, (a, b) in enumerate(zip(sources, held))]
+        ).T
+        for half in range(2)
+    ]
+
+
+def fetches(sources, held, sems):
+    return [pltpu.make_async_copy(a, b, sems.at[i]) for i, (a, b) in enumerate(zip(sources, held))]
+
+
+def pack_kernel(*refs):
+    sources, out_ref, held, turned, sems = refs[:5], refs[5], refs[6:11], refs[11], refs[12]
+    copies = fetches(sources, held, sems)
     for copy in copies:
         copy.start()
     for copy in copies:
         copy.wait()
-
-
-def pack_kernel(*refs):
-    sources, out_ref, held, turned, sems = refs[:5], refs[5], refs[6:11], refs[11], refs[12]
-    fetch(sources, held, sems)
     v_ref, coords_ref, diag_ref, rows_ref, signs_ref = held
     zeros = jnp.zeros((11, 128), F32)
     for jb in range(8):
@@ -108,21 +110,25 @@
             ]
         turned[pl.ds(jb * 128, 128), :] = jnp.concatenate(tiles, 0).T
     lane = lax.broadcasted_iota(jnp.int32, (32, 128), 1)
-    for jt in range(4):
-        made = {}
-        for s in range(LEAF):
-            rows = turned[pl.ds(s, 32, stride=32), :]
-            for col, start, at in (
-                (s // 8, jt * 32, 16 * (s % 8)),
-                (4 + s // 16, jt * 32 + 16, 8 * (s % 16)),
-            ):
-                shift = (at - start) % 128
-                moved = pltpu.roll(rows, shift, 1) if shift else rows
-                if col in made:
-                    moved = jnp.where(lane >= at, moved, made[col])
-                made[col] = moved
-        for col, rows in made.items():
-            out_ref[pl.ds(jt * 32 * OUT_ROWS + col, 32, stride=OUT_ROWS), :] = rows
+    made = {}
+    for s in range(LEAF):
+        rows = turned[pl.ds(s, 32, stride=32), :]
+        for col, start, width, at in (
+            (s // 8, 0, 16, 16 * (s % 8)),
+            (4 + s // 16, 16, 8, 8 * (s % 16)),
+        ):
+            moved = pltpu.roll(rows, at, 1) if at else rows
+            for jt in range(4):
+                first = (jt * 32 + start + at) % 128
+                if (col, jt) in made:
+                    moved_here = jnp.where((lane & -width) == first, moved, made[col, jt])
+                else:
+                    moved_here = moved
+                made[col, jt] = moved_here
+    for (col, jt), rows in made.items():
+        shift = (-jt * 32 - (16 if col >= 4 else 0)) % 128
+        rows = pltpu.roll(rows, shift, 1) if shift else rows
+        out_ref[pl.ds(jt * 32 * OUT_ROWS + col, 32, stride=OUT_ROWS), :] = rows
 
 
 def product(out_count, terms, store, start=None, width=16, group=8):
@@ -162,7 +168,7 @@
 def leaf_kernel(info_ref, got_ref, after_ref, coeffs_ref, leaf_ref, points_ref):
     for c in range(6):
         points_ref[pl.ds(c * 128, 128), :] = got_ref[pl.ds(c, 128, stride=OUT_ROWS), :].T
-    scale = info_ref[0]
+    scale = info_ref[0:1, :]
 
     def powers(field):
         where = points_ref[pl.ds(512 + field, 32, stride=8), :].astype(jnp.int32)
@@ -216,7 +222,7 @@
 
 
 def section_maps(info_ref, k, maps_ref):
-    scale, chip, core = info_ref[0], info_ref[1], info_ref[2]
+    scale, chip, core = info_ref[0:1, :], info_ref[1:2, :], info_ref[2:3, :]
     place = ((chip >> 2) & 7) * 16 + (chip >> 5) * 4 + (chip & 3)
     lane = lax.broadcasted_iota(jnp.int32, (1, 128), 1)
     key = ((lane * 2 + core) * 128 + place) * 37 + 101 * k
@@ -231,23 +237,40 @@
 
 
 def early_kernel(info_ref, *refs):
-    sources, maps_ref, sketch_ref, done_ref = refs[:3], *refs[3:6]
-    held, lhs, rhs, sems = refs[6:9], *refs[9:]
-    fetch(sources, held, sems)
+    sources, maps_hbm, keep_ref, give_ref = refs[:3], *refs[3:6]
+    held, maps, lhs, rhs, sems, map_sems = refs[6:9], *refs[9:]
+    copies = fetches(sources, held, sems)
+    for copy in copies:
+        copy.start()
+
+    def leave(k):
+        return pltpu.make_async_copy(maps.at[k & 1], maps_hbm.at[k - 1], map_sems.at[k & 1])
+
+    def section(k, carry):
+        @pl.when(k > 2)
+        def _():
+            leave(k - 2).wait()
+
+        section_maps(info_ref, k, maps.at[k & 1])
+        leave(k).start()
+        return carry
+
+    lax.fori_loop(1, SECTIONS, section, 0)
+    for copy in copies:
+        copy.wait()
     v_ref, rows_ref, signs_ref = held
-
-    def section(k, carry):
-        section_maps(info_ref, k, maps_ref.at[k - 1])
-        return carry
-
-    lax.fori_loop(1, SECTIONS, section, 0)
     for j in range(32):
         cols = pl.ds(j * 128, 128)
         rows, signs = rows_ref[j : j + 1, :], signs_ref[j : j + 1, :]
         split_rows(lhs, v_ref[:, cols] * (2 * signs - 1).astype(F32), rows >> 8, cols)
         hot_rows(rhs, rows & 255, cols)
-    sketched(lhs, rhs, sketch_ref, 0, 2)
-    done_ref[...] = jnp.zeros((8, 128), F32)
+    low, high = sketched(lhs, rhs)
+    first = info_ref[2:3, :] == 0
+    first = jnp.broadcast_to(first, (128, 128))
+    keep_ref[...] = jnp.where(first, low, high)
+    give_ref[...] = jnp.where(first, high, low)
+    for k in (SECTIONS - 2, SECTIONS - 1):
+        leave(k).wait()
 
 
 def hot_kernel(info_ref, points_ref, rhs_ref, maps_ref):
@@ -264,9 +287,11 @@
     points_ref,
     first,
     rhs,
-    vsketch_ref,
+    keep_ref,
+    taken_ref,
     maps_hbm,
     out_ref,
+    image_ref,
     now,
     other,
     image,
@@ -354,13 +379,13 @@
         energy += r * r
         mixed += r * v
     for c in range(4):
-        out_ref[pl.ds(c, 128, stride=BACK_ROWS), :] = image[pl.ds(c * 128, 128), :].T
-    for c in range(2):
-        out_ref[pl.ds(6 + c, 128, stride=BACK_ROWS), :] = vsketch_ref[pl.ds(c, 128, stride=2), :]
-    sketched(lhs, rhs, out_ref, 4, BACK_ROWS)
+        image_ref[pl.ds(c * 128, 128), :] = image[pl.ds(c * 128, 128), :].T
+    for half, tile in enumerate(sketched(lhs, rhs)):
+        out_ref[pl.ds(half, 128, stride=SUM_ROWS), :] = tile
+    out_ref[pl.ds(2, 128, stride=SUM_ROWS), :] = keep_ref[...] + taken_ref[...]
     rest = jnp.where(lane < 32, state_rows([energy, mixed]), 0.0)
     state = vv + pltpu.roll(local, 16, 1) + pltpu.roll(rest, 32, 1)
-    out_ref[pl.ds(8, 128, stride=BACK_ROWS), :] = jnp.broadcast_to(state, (128, 128))
+    out_ref[pl.ds(3, 128, stride=SUM_ROWS), :] = jnp.broadcast_to(state, (128, 128))
 
 
 def merged(vv, p, e, cr, total):
@@ -375,12 +400,17 @@
     return total(e + off * (2.0 * cr + off * vv)), total(cr + off * vv)
 
 
-def sum_kernel(got_ref, out_ref):
-    for c in range(4):
-        out_ref[c : c + 1, :] = jnp.sum(
-            got_ref[pl.ds(4 + c, 128, stride=BACK_ROWS), :], axis=0, keepdims=True
-        )
-    state = got_ref[pl.ds(8, 128, stride=BACK_ROWS), :]
+def sum_kernel(info_ref, got_ref, out_ref):
+    sums = [
+        jnp.sum(got_ref[pl.ds(c, 128, stride=SUM_ROWS), :], axis=0, keepdims=True)
+        for c in range(3)
+    ]
+    first = info_ref[2:3, :] == 0
+    out_ref[0:1, :] = sums[0]
+    out_ref[1:2, :] = sums[1]
+    out_ref[2:3, :] = jnp.where(first, sums[2], 0.0)
+    out_ref[3:4, :] = jnp.where(first, 0.0, sums[2])
+    state = got_ref[pl.ds(3, 128, stride=SUM_ROWS), :]
     valid = lax.broadcasted_iota(jnp.int32, (128, 128), 1) < 16
     parts = [
         jnp.where(valid, pltpu.roll(state, (128 - 16 * i) % 128, 1) if i else state, 0.0)
@@ -396,7 +426,9 @@
         out_ref[4 + i : 5 + i, :] = x
 
 
-def chunk_kernel(mine_ref, theirs_ref, chunk_ref, arnoldi_ref, scalars_ref):
+def chunk_kernel(mine_ref, theirs_ref, image_ref, out_ref, arnoldi_ref, scalars_ref):
+    for c in range(4):
+        out_ref[pl.ds(c, 128, stride=BACK_ROWS), :] = image_ref[pl.ds(c * 128, 128), :]
     both = [(mine_ref[4 + i : 5 + i, :], theirs_ref[4 + i : 5 + i, :]) for i in range(4)]
     vv, p, e, cr = both
     square = vv[0] + vv[1]
@@ -423,38 +455,39 @@
     sums = mine_ref[0:4, :] + theirs_ref[0:4, :]
     chunk = (sums[0:2] - proj * sums[2:4]) / spread * math.sqrt(SKETCH / NPTS)
     for i in range(2):
-        chunk_ref[pl.ds(i, 128, stride=2), :] = jnp.broadcast_to(chunk[i : i + 1], (128, 128))
-
-
-def basis_kernel(got_ref, scalars_ref, v_ref, basis_ref, turned):
+        out_ref[pl.ds(4 + i, 128, stride=BACK_ROWS), :] = jnp.broadcast_to(
+            chunk[i : i + 1], (128, 128)
+        )
+
+
+def last_kernel(got_ref, scalars_ref, v_ref, basis_ref, sketch_ref, turned):
     proj = jnp.broadcast_to(scalars_ref[0:1, :], (128, 128)).T[0:NRHS, :]
     spread = jnp.broadcast_to(scalars_ref[1:2, :], (128, 128)).T[0:NRHS, :]
-    lane = lax.broadcasted_iota(jnp.int32, (32, 128), 1)
-    for s in range(LEAF):
-        made = None
+    lane = lax.broadcasted_iota(jnp.int32, (32, 128), 1) & -16
+    for c in range(4):
+        blocks = []
         for jt in range(4):
-            rows = got_ref[pl.ds(jt * 32 * BACK_ROWS + s // 8, 32, stride=BACK_ROWS), :]
-            shift = (jt * 32 - (s % 8) * 16) % 128
-            rows = pltpu.roll(rows, shift, 1) if shift else rows
-            made = rows if made is None else jnp.where(lane >= jt * 32, rows, made)
-        turned[pl.ds(s, 32, stride=32), :] = made
+            rows = got_ref[pl.ds(jt * 32 * BACK_ROWS + c, 32, stride=BACK_ROWS), :]
+            blocks.append(pltpu.roll(rows, jt * 32, 1) if jt else rows)
+        for m in range(8):
+            made = blocks[0]
+            for jt in range(1, 4):
+                made = jnp.where(lane == (jt * 32 + m * 16) % 128, blocks[jt], made)
+            made = pltpu.roll(made, 128 - m * 16, 1) if m else made
+            turned[pl.ds(c * 8 + m, 32, stride=32), :] = made
     for jb in range(8):
         back = turned[pl.ds(jb * 128, 128), :].T
         for jt in range(4):
             cols = pl.ds((jb * 4 + jt) * 128, 128)
             x = back[jt * 32 : jt * 32 + 16, :]
             basis_ref[:, cols] = (x - proj * v_ref[:, cols]) / spread
-
-
-def spread_kernel(got_ref, out_ref):
     for half in range(2):
-        tile = got_ref[pl.ds(half, 128, stride=2), :].T
+        tile = got_ref[pl.ds(4 + half, 128, stride=BACK_ROWS), :].T
         for t in range(8):
-            out_ref[:, pl.ds((half * 8 + t) * 128, 128)] = tile[t * 16 : t * 16 + 16, :]
+            sketch_ref[:, pl.ds((half * 8 + t) * 128, 128)] = tile[t * 16 : t * 16 + 16, :]
 
 
 VMEM = pl.BlockSpec(memory_space=pltpu.VMEM)
-SMEM = pl.BlockSpec(memory_space=pltpu.SMEM)
 HBM = pl.BlockSpec(memory_space=pltpu.HBM)
 
 
@@ -462,13 +495,13 @@
     return jax.ShapeDtypeStruct(shape, F32)
 
 
-def call(kernel, out, ins, scratch=(), flops=1000000, mib=12):
+def call(kernel, out, ins, scratch=(), flops=1000000, mib=12, outs=None):
     single = not isinstance(out, tuple)
     return pl.pallas_call(
         kernel,
         out_shape=out,
         in_specs=ins,
-        out_specs=VMEM if single else tuple(VMEM for _ in out),
+        out_specs=outs or (VMEM if single else tuple(VMEM for _ in out)),
         scratch_shapes=list(scratch),
         cost_estimate=pl.CostEstimate(flops=flops, bytes_accessed=1000000, transcendentals=0),
         compiler_params=pltpu.CompilerParams(vmem_limit_bytes=mib * 1024 * 1024),
@@ -482,7 +515,8 @@
 def body(basis_vector, diagonal, coords, phase_scale, sketch_rows, sketch_signs):
     chip = lax.axis_index(CHIP)
     core = lax.axis_index(CORE)
-    info = jnp.stack([phase_scale[0] % MOD, chip, core]).astype(jnp.int32)
+    info = jnp.stack([phase_scale[0] % MOD, chip, core] + [core] * 5).astype(jnp.int32)
+    info = jnp.broadcast_to(info[:, None], (8, 128))
     points = LEAF * CHIPS
     swap = [(0, 1), (1, 0)]
     sketch_rows, sketch_signs = sketch_rows.reshape(32, 128), sketch_signs.reshape(32, 128)
@@ -506,49 +540,59 @@
         ],
         mib=60,
     )(basis_vector, coords, diagonal.reshape(32, 128), sketch_rows, sketch_signs)
-    maps, vsketch, done = call(
+    map_pair = pltpu.VMEM((2, 2, WIDTH, WIDTH, 128), F32)
+    tile = f32(CHIPS, 128)
+    maps, keep, give = call(
         early_kernel,
-        (f32(SECTIONS - 1, 2, WIDTH, WIDTH, 128), f32(CHIPS * 2, 128), f32(8, 128)),
-        [SMEM] + [HBM] * 3,
-        [vector, ints, ints, parts, parts, pltpu.SemaphoreType.DMA((3,))],
+        (f32(SECTIONS - 1, 2, WIDTH, WIDTH, 128), tile, tile),
+        [VMEM] + [HBM] * 3,
+        [
+            vector,
+            ints,
+            ints,
+            map_pair,
+            parts,
+            parts,
+            pltpu.SemaphoreType.DMA((3,)),
+            pltpu.SemaphoreType.DMA((2,)),
+        ],
+        outs=(HBM, VMEM, VMEM),
         flops=20000000,
         mib=EARLY_MIB,
     )(info, basis_vector, sketch_rows, sketch_signs)
     got = exchange(packed)
+    taken = lax.ppermute(give, CORE, swap)
     coeffs, leaf, held = call(
         leaf_kernel,
         (f32(512, 128), f32(WIDTH, LEAF, 128), f32(OUT_ROWS * 128, 128)),
-        [SMEM, VMEM, HBM],
-    )(info, got, done)
+        [VMEM, VMEM, HBM],
+    )(info, got, keep)
     partner = lax.ppermute(coeffs, CORE, swap)
     first_type = f32(2, WIDTH, WIDTH, 128)
-    hot, first = call(hot_kernel, (hot_type, first_type), [SMEM, VMEM])(info, held)
+    hot, first = call(hot_kernel, (hot_type, first_type), [VMEM, VMEM])(info, held)
     pair = pltpu.VMEM((2, 512, 128), F32)
-    back = call(
+    parts_out, image = call(
         core_kernel,
-        f32(CHIPS * BACK_ROWS, 128),
-        [VMEM] * 7 + [HBM],
+        (f32(CHIPS * SUM_ROWS, 128), f32(512, 128)),
+        [VMEM] * 8 + [HBM],
         [
             pair,
             pair,
             pltpu.VMEM((512, 128), F32),
             parts,
-            pltpu.VMEM((2, 2, WIDTH, WIDTH, 128), F32),
+            map_pair,
             pltpu.SemaphoreType.DMA((2,)),
         ],
         mib=CORE_MIB,
-    )(coeffs, partner, leaf, held, first, hot, vsketch, maps)
-    home = exchange(back)
-    mine = call(sum_kernel, f32(8, 128), [VMEM])(home)
+    )(coeffs, partner, leaf, held, first, hot, keep, taken, maps)
+    mine = call(sum_kernel, f32(8, 128), [VMEM, VMEM])(info, exchange(parts_out))
     theirs = lax.ppermute(mine, CORE, swap)
-    chunk, arnoldi, scalars = call(
-        chunk_kernel, (f32(CHIPS * 2, 128), f32(2, NRHS), f32(2, 128)), [VMEM] * 2
-    )(mine, theirs)
-    spread = exchange(chunk)
-    new_basis = call(basis_kernel, f32(NRHS, points), [VMEM] * 3, [turned], flops=20000000)(
-        home, scalars, basis_vector
-    )
-    sketch = call(spread_kernel, f32(NRHS, SKETCH), [VMEM])(spread)
+    back, arnoldi, scalars = call(
+        chunk_kernel, (f32(CHIPS * BACK_ROWS, 128), f32(2, NRHS), f32(2, 128)), [VMEM] * 3
+    )(mine, theirs, image)
+    new_basis, sketch = call(
+        last_kernel, (f32(NRHS, points), f32(NRHS, SKETCH)), [VMEM] * 3, [turned]
+    )(exchange(back), scalars, basis_vector)
     return new_basis, sketch, arnoldi
 
 

time: 104 us -> 99.6 us (0.958)
  blocking collectives: 25.3 us -> 40 us
  waiting for transfers between devices: 14.7 us -> 7.04 us
  starting transfers between devices: 29.2 us -> 22.3 us
  local copies, waits for them, and re-layouts: 5.33 us -> 2.55 us
  Pallas kernels: 27.4 us -> 26 us
    all_to_all x1 -> x2, blocking collectives: 25.3 us -> 40 us  [exchange(): return lax.all_to_all(x[:, None, :], CHIP, 0, 0, tiled=True)[:, 0, :]]
    all_to_all x2 -> x1, waiting for transfers between devices: 13.9 us -> 5.84 us  [exchange(): return lax.all_to_all(x[:, None, :], CHIP, 0, 0, tiled=True)[:, 0, :]]
    all_to_all x2 -> x1, starting transfers between devices: 23.6 us -> 16.3 us  [exchange(): return lax.all_to_all(x[:, None, :], CHIP, 0, 0, tiled=True)[:, 0, :]]
    unnamed x10 -> x8, local copies, waits for them, and re-layouts: 5.33 us -> 2.39 us
    pallas_call x7 -> x6, Pallas kernels: 22.7 us -> 22.6 us  [the longest x1 13.6 us: body(): call(core_kernel, (f32(CHIPS * SUM_ROWS, 128), f32(512, 128)), [VMEM] * 8...]
where the time goes in v3:
time: 99.6 us; the launch traced here: 99.2 us
  blocking collectives  40 us (40%)
  Pallas kernels  26 us (26%)
  starting transfers between devices  22.3 us (22%)
  waiting for transfers between devices  7.04 us (7%)
  local copies, waits for them, and re-layouts  2.55 us (3%)
  between operations  1.37 us (1%)
    all_to_all x2, blocking collectives, exchange(): return lax.all_to_all(x[:, None, :], CHIP, 0, 0, tiled=True)[:, 0, :]  40 us
    all_to_all x1, starting transfers between devices, exchange(): return lax.all_to_all(x[:, None, :], CHIP, 0, 0, tiled=True)[:, 0, :]  16.3 us
    pallas_call x1, Pallas kernels, body(): call(core_kernel, (f32(CHIPS * SUM_ROWS, 128), f32(512, 128)), [VMEM] * 8...  13.6 us
    pallas_call x1, Pallas kernels, body(): call(early_kernel, (f32(SECTIONS - 1, 2, WIDTH, WIDTH, 128), tile, tile),...  5.92 us
    all_to_all x1, waiting for transfers between devices, exchange(): return lax.all_to_all(x[:, None, :], CHIP, 0, 0, tiled=True)[:, 0, :]  5.84 us
    ppermute x1, starting transfers between devices, body(): partner = lax.ppermute(coeffs, CORE, swap)  3.1 us
    ppermute x1, starting transfers between devices, body(): theirs = lax.ppermute(mine, CORE, swap)  2.72 us
    pallas_call x1, Pallas kernels, body(): call(pack_kernel, f32(CHIPS * OUT_ROWS, 128), [HBM] * 5, [vector, pltpu.V...  2.46 us
  transfers between devices with their start and end apart: 4, of which 3 were waited for; matrix products, arithmetic and copies ran while one was open for 0% of the time, Pallas kernels for 7%

profile of v3, /device:TPU:1, one launch (start us, length us, event | category | flops | bytes accessed | tf_op | source)
XLA Modules:
  0.0 99.2 jit_solution(16928444313504796618)
XLA Ops:
  0.6 2.5 %shard_map.85 = f32[768,128]{1,0:T(8,128)} custom-call(f32[16,4096]{1,0:T(8,128)} %v_ref.1, s32[2,4096]{1,0:T(2,128)} %refs_1_.1, f32[32,128]{1,0:T(8,128)} %bitcast.29, s32[32,128]{1,0:T(8,128)} %bitcast.24, s32[32,128]{1,0:T(8,128)} %bitcast.26), custom_call_target="tpu_custom_call" | custom-call | flops 1000000 | bytes 1000000 | tf_op jit(solution)/shard_map/pallas_call | solution.py:528
  3.1 16.3 %all-to-all-start = ((f32[768,1,128]{2,1,0:T(1,128)}), f32[768,1,128]{2,1,0:T(1,128)S(1)}, u32[]{:S(2)}, u32[]{:S(2)}) async-start(f32[768,1,128]{2,1,0:T(1,128)} %bitcast.28), calls=%async_computation | async-start | bytes 786432 | tf_op jit(solution)/shard_map/all_to_all | solution.py:512
  20.1 0.1 stack.20
  20.2 0.1 broadcast_in_dim.15.info_ref
  20.3 1.0 copy-done
  21.2 0.7 copy-done.2
  21.9 0.7 copy-done.3
  22.7 5.9 %shard_map.86 = (f32[7,2,32,32,128]{4,3,2,1,0:T(8,128)}, f32[128,128]{1,0:T(8,128)S(1)}, f32[128,128]{1,0:T(8,128)S(1)}) custom-call(s32[8,128]{1,0:T(8,128)S(1)} %broadcast_in_dim.15.info_ref, f32[16,4096]{1,0:T(8,128)S(1)} %copy-done, s32[32,128]{1,0:T(8,128)S(1)} %bitcast.25, s32[32,128]{1,0:T(8,128)S(1)} %bitcast.27), custom_call_target="tpu_custom_call" | custom-call | flops 20000000 | bytes 1000000 | tf_op jit(solution)/shard_map/pallas_call | solution.py:545
  28.6 5.8 %all-to-all-done = f32[768,1,128]{2,1,0:T(1,128)S(1)} async-done(((f32[768,1,128]{2,1,0:T(1,128)}), f32[768,1,128]{2,1,0:T(1,128)S(1)}, u32[]{:S(2)}, u32[]{:S(2)}) %all-to-all-start) | async-done | bytes 393248 | tf_op jit(solution)/shard_map/all_to_all | solution.py:512
  34.4 0.9 shard_map.87
  35.4 3.1 %collective-permute-start = (f32[512,128]{1,0:T(8,128)S(1)}, f32[512,128]{1,0:T(8,128)S(1)}, u32[]{:S(2)}, u32[]{:S(2)}) collective-permute-start(f32[512,128]{1,0:T(8,128)S(1)} %get-tuple-element.19.coeffs_ref), channel_id=1, source_target_pairs={{0,1},{1,0},{2,3},{3,2},{4,5},{5,4},{6,7},{7,6},{8,9},{9,8},{10,11... | collective-permute-start | bytes 786440 | tf_op jit(solution)/shard_map/ppermute | solution.py:570
  38.5 0.1 collective-permute-start.1
  38.6 0.8 shard_map.88
  39.4 0.4 collective-permute-done.1.taken_ref
  39.7 0.0 collective-permute-done.partner_ref
  39.7 13.6 %shard_map.89 = (f32[512,128]{1,0:T(8,128)S(1)}, f32[512,128]{1,0:T(8,128)S(1)}) custom-call(f32[512,128]{1,0:T(8,128)S(1)} %get-tuple-element.19.coeffs_ref, f32[512,128]{1,0:T(8,128)S(1)} %collective-permute-done.partner_ref, f32[32,32,128]{2,1,0:T(8,128)S(1)} %get-tuple-element.20.leaf_ref, f32[768,128]{1,0:T(8,128)S(1)} %get-tuple-element.21.points_ref, ...), custom_call_target="tpu_custom_call" | custom-call | flops 1000000 | bytes 1000000 | tf_op jit(solution)/shard_map/pallas_call | solution.py:574
  53.4 18.9 %all_to_all.15 = f32[512,1,128]{2,1,0:T(1,128)S(1)} all-to-all(f32[512,1,128]{2,1,0:T(1,128)S(1)} %bitcast.23), channel_id=1, replica_groups=mesh['box_0'=4,'box_1'=8,'box_2'=4,'box_3'=2] {'box_0','box_1','box_2'}, dimensions={0} | all-to-all | bytes 524288 | tf_op jit(solution)/shard_map/all_to_all | solution.py:512
  72.3 0.1 shard_map.90.mine_ref
  72.4 2.7 %collective-permute-start.2 = (f32[8,128]{1,0:T(8,128)S(1)}, f32[8,128]{1,0:T(8,128)S(1)}, u32[]{:S(2)}, u32[]{:S(2)}) collective-permute-start(f32[8,128]{1,0:T(8,128)S(1)} %shard_map.90.mine_ref), channel_id=1, source_target_pairs={{0,1},{1,0},{2,3},{3,2},{4,5},{5,4},{6,7},{7,6},{8,9},{9,8},{10,11... | collective-permute-start | bytes 12296 | tf_op jit(solution)/shard_map/ppermute | solution.py:589
  75.1 0.8 collective-permute-done.2.theirs_ref
  76.0 0.6 shard_map.91
  76.5 21.0 %all_to_all.16 = f32[768,1,128]{2,1,0:T(1,128)S(1)} all-to-all(f32[768,1,128]{2,1,0:T(1,128)S(1)} %bitcast.22), channel_id=1, replica_groups=mesh['box_0'=4,'box_1'=8,'box_2'=4,'box_3'=2] {'box_0','box_1','box_2'}, dimensions={0} | all-to-all | bytes 786432 | tf_op jit(solution)/shard_map/all_to_all | solution.py:512
  97.6 0.0 copy-done.1
  97.6 1.6 %shard_map.92 = (f32[16,4096]{1,0:T(8,128)}, f32[16,2048]{1,0:T(8,128)}) custom-call(f32[768,128]{1,0:T(8,128)S(1)} %bitcast.20, f32[2,128]{1,0:T(2,128)S(1)} %get-tuple-element.29.scalars_ref, f32[16,4096]{1,0:T(8,128)S(1)} %copy-done.1), custom_call_target="tpu_custom_call" | custom-call | flops 1000000 | bytes 1000000 | tf_op jit(solution)/shard_map/pallas_call | solution.py:593
  (4 shorter events, 0.0 us)
Async XLA Ops:
  3.1 31.3 %all-to-all-start = ((f32[768,1,128]{2,1,0:T(1,128)}), f32[768,1,128]{2,1,0:T(1,128)S(1)}, u32[]{:S(2)}, u32[]{:S(2)}) async-start(f32[768,1,128]{2,1,0:T(1,128)} %bitcast.28), calls=%async_computation | async-start | bytes 786432 | tf_op jit(solution)/shard_map/all_to_all | solution.py:512
  20.3 1.0 copy-start
  21.2 0.7 copy-start.2
  21.9 0.7 copy-start.3
  34.4 63.1 %copy-start.1 = (f32[16,4096]{1,0:T(8,128)S(1)}, f32[16,4096]{1,0:T(8,128)}, u32[]{:S(2)}) copy-start(f32[16,4096]{1,0:T(8,128)} %v_ref.1) | copy-start | bytes 786436
  35.4 4.4 %collective-permute-start = (f32[512,128]{1,0:T(8,128)S(1)}, f32[512,128]{1,0:T(8,128)S(1)}, u32[]{:S(2)}, u32[]{:S(2)}) collective-permute-start(f32[512,128]{1,0:T(8,128)S(1)} %get-tuple-element.19.coeffs_ref), channel_id=1, source_target_pairs={{0,1},{1,0},{2,3},{3,2},{4,5},{5,4},{6,7},{7,6},{8,9},{9,8},{10,11... | collective-permute-start | bytes 786440 | tf_op jit(solution)/shard_map/ppermute | solution.py:570
  38.5 1.3 %collective-permute-start.1 = (f32[128,128]{1,0:T(8,128)S(1)}, f32[128,128]{1,0:T(8,128)S(1)}, u32[]{:S(2)}, u32[]{:S(2)}) collective-permute-start(f32[128,128]{1,0:T(8,128)S(1)} %get-tuple-element.24), channel_id=1, source_target_pairs={{0,1},{1,0},{2,3},{3,2},{4,5},{5,4},{6,7},{7,6},{8,9},{9,8},{10,11... | collective-permute-start | bytes 196616 | tf_op jit(solution)/shard_map/ppermute | solution.py:564
  72.4 3.5 %collective-permute-start.2 = (f32[8,128]{1,0:T(8,128)S(1)}, f32[8,128]{1,0:T(8,128)S(1)}, u32[]{:S(2)}, u32[]{:S(2)}) collective-permute-start(f32[8,128]{1,0:T(8,128)S(1)} %shard_map.90.mine_ref), channel_id=1, source_target_pairs={{0,1},{1,0},{2,3},{3,2},{4,5},{5,4},{6,7},{7,6},{8,9},{9,8},{10,11... | collective-permute-start | bytes 12296 | tf_op jit(solution)/shard_map/ppermute | solution.py:589

commit v4 on v3

--- a/solution.py
+++ b/solution.py
@@ -131,7 +131,7 @@
         out_ref[pl.ds(jt * 32 * OUT_ROWS + col, 32, stride=OUT_ROWS), :] = rows
 
 
-def product(out_count, terms, store, start=None, width=16, group=8):
+def product(out_count, terms, store, start=None, width=16, group=16):
     def tile(t, carry):
         accs = [jnp.zeros((8, 128), F32)] * (2 * width)
         if start is not None:
@@ -300,25 +300,26 @@
     sems,
 ):
     lane = lax.broadcasted_iota(jnp.int32, (1, 128), 1)
-    lanes = lax.broadcasted_iota(jnp.int32, (NRHS, 128), 1)
+    lanes = lax.broadcasted_iota(jnp.int32, (8, 128), 1)
 
     def copy(k):
-        return pltpu.make_async_copy(maps_hbm.at[k - 1], maps.at[k & 1], sems.at[k & 1])
-
-    copy(1).start()
+        slot = lax.rem(k, 3)
+        return pltpu.make_async_copy(maps_hbm.at[k - 1], maps.at[slot], sems.at[slot])
+
+    copy(jnp.int32(1)).start()
+    copy(jnp.int32(2)).start()
     now[0] = coeffs_ref[...]
     other[0] = partner_ref[...]
 
     def section(k, own, cross):
         at = k & 1
         step = jnp.left_shift(1, jnp.minimum(k, SECTIONS - 2))
-        bit = (lanes & step) == 0
+        across = lanes ^ step
 
         def store(a, x):
-            x = jnp.concatenate(x, 0)
-            now[1 - at, row16(a), :] = x
-            other[1 - at, row16(a), :] = jnp.where(
-                bit, pltpu.roll(x, 128 - step, 1), pltpu.roll(x, step, 1)
+            now[1 - at, row16(a), :] = jnp.concatenate(x, 0)
+            other[1 - at, row16(a), :] = jnp.concatenate(
+                [jnp.take_along_axis(y, across, axis=1, mode="promise_in_bounds") for y in x], 0
             )
 
         product(
@@ -336,35 +337,36 @@
     def later(k, carry):
         copy(k).wait()
 
-        @pl.when(k < SECTIONS - 1)
+        @pl.when(k < SECTIONS - 2)
         def _():
-            copy(k + 1).start()
-
-        section(k, maps.at[k & 1, 0], maps.at[k & 1, 1])
+            copy(k + 2).start()
+
+        slot = lax.rem(k, 3)
+        section(k, maps.at[slot, 0], maps.at[slot, 1])
         return carry
 
     lax.fori_loop(1, SECTIONS, later, 0)
 
+    def apply(s, x):
+        at = pl.multiple_of(512 + s * 8, 8)
+        diagonal = points_ref[pl.ds(at, 8), :][2:3, :]
+        image[row16(s), :] = diagonal * points_ref[row16(s), :] + jnp.concatenate(x, 0)
+
+    product(
+        LEAF,
+        [(lambda a, b: leaf_ref[b, pl.ds(a, 1), :], lambda b: halves(now, b, 0))],
+        apply,
+    )
     square = jnp.zeros((NRHS, 128), F32)
     inner = jnp.zeros((NRHS, 128), F32)
-    for t in range(2):
-        accs = [None] * 16
-        for w in range(WIDTH):
-            vec = now[0, pl.ds(w * 16, 16), :]
-            for i in range(16):
-                s = t * 16 + i
-                term = leaf_ref[w, s : s + 1, :] * vec
-                accs[i] = term if accs[i] is None else accs[i] + term
-        for i in range(16):
-            s = t * 16 + i
-            v = points_ref[pl.ds(s * 16, 16), :]
-            x = points_ref[pl.ds(512 + s * 8 + 2, 1), :] * v + accs[i]
-            image[pl.ds(s * 16, 16), :] = x
-            square += v * v
-            inner += v * x
-            sign = 2.0 * points_ref[pl.ds(512 + s * 8 + 4, 1), :] - 1.0
-            high = points_ref[pl.ds(512 + s * 8 + 3, 1), :].astype(jnp.int32) >> 8
-            split_rows(lhs, x * sign, high, pl.ds(s * 128, 128))
+    for s in range(LEAF):
+        v = points_ref[pl.ds(s * 16, 16), :]
+        x = image[pl.ds(s * 16, 16), :]
+        square += v * v
+        inner += v * x
+        sign = 2.0 * points_ref[pl.ds(512 + s * 8 + 4, 1), :] - 1.0
+        high = points_ref[pl.ds(512 + s * 8 + 3, 1), :].astype(jnp.int32) >> 8
+        split_rows(lhs, x * sign, high, pl.ds(s * 128, 128))
     sums = state_rows([square, inner])
     valid = lane < 16
     vv = jnp.where(valid, sums, 0.0)
@@ -460,9 +462,15 @@
         )
 
 
-def last_kernel(got_ref, scalars_ref, v_ref, basis_ref, sketch_ref, turned):
+def last_kernel(got_ref, scalars_ref, v_ref, basis_hbm, sketch_hbm, turned, basis_ref, sketch_ref, sems):
+    for half in range(2):
+        tile = got_ref[pl.ds(4 + half, 128, stride=BACK_ROWS), :].T
+        for t in range(8):
+            sketch_ref[:, pl.ds((half * 8 + t) * 128, 128)] = tile[t * 16 : t * 16 + 16, :]
+    copies = [pltpu.make_async_copy(sketch_ref, sketch_hbm, sems.at[8])]
+    copies[0].start()
     proj = jnp.broadcast_to(scalars_ref[0:1, :], (128, 128)).T[0:NRHS, :]
-    spread = jnp.broadcast_to(scalars_ref[1:2, :], (128, 128)).T[0:NRHS, :]
+    gain = jnp.broadcast_to(1.0 / scalars_ref[1:2, :], (128, 128)).T[0:NRHS, :]
     lane = lax.broadcasted_iota(jnp.int32, (32, 128), 1) & -16
     for c in range(4):
         blocks = []
@@ -480,11 +488,14 @@
         for jt in range(4):
             cols = pl.ds((jb * 4 + jt) * 128, 128)
             x = back[jt * 32 : jt * 32 + 16, :]
-            basis_ref[:, cols] = (x - proj * v_ref[:, cols]) / spread
-    for half in range(2):
-        tile = got_ref[pl.ds(4 + half, 128, stride=BACK_ROWS), :].T
-        for t in range(8):
-            sketch_ref[:, pl.ds((half * 8 + t) * 128, 128)] = tile[t * 16 : t * 16 + 16, :]
+            basis_ref[:, cols] = (x - proj * v_ref[:, cols]) * gain
+        cols = pl.ds(jb * 512, 512)
+        copies.append(
+            pltpu.make_async_copy(basis_ref.at[:, cols], basis_hbm.at[:, cols], sems.at[jb])
+        )
+        copies[-1].start()
+    for copy in copies:
+        copy.wait()
 
 
 VMEM = pl.BlockSpec(memory_space=pltpu.VMEM)
@@ -580,8 +591,8 @@
             pair,
             pltpu.VMEM((512, 128), F32),
             parts,
-            map_pair,
-            pltpu.SemaphoreType.DMA((2,)),
+            pltpu.VMEM((3, 2, WIDTH, WIDTH, 128), F32),
+            pltpu.SemaphoreType.DMA((3,)),
         ],
         mib=CORE_MIB,
     )(coeffs, partner, leaf, held, first, hot, keep, taken, maps)
@@ -591,7 +602,11 @@
         chunk_kernel, (f32(CHIPS * BACK_ROWS, 128), f32(2, NRHS), f32(2, 128)), [VMEM] * 3
     )(mine, theirs, image)
     new_basis, sketch = call(
-        last_kernel, (f32(NRHS, points), f32(NRHS, SKETCH)), [VMEM] * 3, [turned]
+        last_kernel,
+        (f32(NRHS, points), f32(NRHS, SKETCH)),
+        [VMEM] * 3,
+        [turned, vector, pltpu.VMEM((NRHS, SKETCH), F32), pltpu.SemaphoreType.DMA((9,))],
+        outs=(HBM, HBM),
     )(exchange(back), scalars, basis_vector)
     return new_basis, sketch, arnoldi
 

time: 99.6 us -> 98.8 us (level)
  no operation moved by 1% of the time
where the time goes in v4:
time: 98.8 us; the launch traced here: 98.3 us
  blocking collectives  40 us (40%)
  Pallas kernels  25.2 us (26%)
  starting transfers between devices  22.3 us (23%)
  waiting for transfers between devices  7.04 us (7%)
  local copies, waits for them, and re-layouts  2.55 us (3%)
  between operations  1.37 us (1%)
    all_to_all x2, blocking collectives, exchange(): return lax.all_to_all(x[:, None, :], CHIP, 0, 0, tiled=True)[:, 0, :]  40 us
    all_to_all x1, starting transfers between devices, exchange(): return lax.all_to_all(x[:, None, :], CHIP, 0, 0, tiled=True)[:, 0, :]  16.3 us
    pallas_call x1, Pallas kernels, body(): call(core_kernel, (f32(CHIPS * SUM_ROWS, 128), f32(512, 128)), [VMEM] * 8...  12.9 us
    pallas_call x1, Pallas kernels, body(): call(early_kernel, (f32(SECTIONS - 1, 2, WIDTH, WIDTH, 128), tile, tile),...  5.92 us
    all_to_all x1, waiting for transfers between devices, exchange(): return lax.all_to_all(x[:, None, :], CHIP, 0, 0, tiled=True)[:, 0, :]  5.84 us
    ppermute x1, starting transfers between devices, body(): partner = lax.ppermute(coeffs, CORE, swap)  3.1 us
    ppermute x1, starting transfers between devices, body(): theirs = lax.ppermute(mine, CORE, swap)  2.72 us
    pallas_call x1, Pallas kernels, body(): call(pack_kernel, f32(CHIPS * OUT_ROWS, 128), [HBM] * 5, [vector, pltpu.V...  2.46 us
  transfers between devices with their start and end apart: 4, of which 3 were waited for; matrix products, arithmetic and copies ran while one was open for 0% of the time, Pallas kernels for 7%

profile of v4, /device:TPU:1, one launch (start us, length us, event | category | flops | bytes accessed | tf_op | source)
XLA Modules:
  0.0 98.3 jit_solution(13749954665762560389)
XLA Ops:
  0.6 2.5 %shard_map.85 = f32[768,128]{1,0:T(8,128)} custom-call(f32[16,4096]{1,0:T(8,128)} %v_ref.1, s32[2,4096]{1,0:T(2,128)} %refs_1_.1, f32[32,128]{1,0:T(8,128)} %bitcast.29, s32[32,128]{1,0:T(8,128)} %bitcast.24, s32[32,128]{1,0:T(8,128)} %bitcast.26), custom_call_target="tpu_custom_call" | custom-call | flops 1000000 | bytes 1000000 | tf_op jit(solution)/shard_map/pallas_call | solution.py:539
  3.1 16.3 %all-to-all-start = ((f32[768,1,128]{2,1,0:T(1,128)}), f32[768,1,128]{2,1,0:T(1,128)S(1)}, u32[]{:S(2)}, u32[]{:S(2)}) async-start(f32[768,1,128]{2,1,0:T(1,128)} %bitcast.28), calls=%async_computation | async-start | bytes 786432 | tf_op jit(solution)/shard_map/all_to_all | solution.py:523
  20.1 0.1 stack.20
  20.2 0.1 broadcast_in_dim.15.info_ref
  20.3 1.0 copy-done
  21.2 0.7 copy-done.2
  21.9 0.7 copy-done.3
  22.7 5.9 %shard_map.86 = (f32[7,2,32,32,128]{4,3,2,1,0:T(8,128)}, f32[128,128]{1,0:T(8,128)S(1)}, f32[128,128]{1,0:T(8,128)S(1)}) custom-call(s32[8,128]{1,0:T(8,128)S(1)} %broadcast_in_dim.15.info_ref, f32[16,4096]{1,0:T(8,128)S(1)} %copy-done, s32[32,128]{1,0:T(8,128)S(1)} %bitcast.25, s32[32,128]{1,0:T(8,128)S(1)} %bitcast.27), custom_call_target="tpu_custom_call" | custom-call | flops 20000000 | bytes 1000000 | tf_op jit(solution)/shard_map/pallas_call | solution.py:556
  28.6 5.8 %all-to-all-done = f32[768,1,128]{2,1,0:T(1,128)S(1)} async-done(((f32[768,1,128]{2,1,0:T(1,128)}), f32[768,1,128]{2,1,0:T(1,128)S(1)}, u32[]{:S(2)}, u32[]{:S(2)}) %all-to-all-start) | async-done | bytes 393248 | tf_op jit(solution)/shard_map/all_to_all | solution.py:523
  34.4 0.9 shard_map.87
  35.3 3.1 %collective-permute-start = (f32[512,128]{1,0:T(8,128)S(1)}, f32[512,128]{1,0:T(8,128)S(1)}, u32[]{:S(2)}, u32[]{:S(2)}) collective-permute-start(f32[512,128]{1,0:T(8,128)S(1)} %get-tuple-element.19.coeffs_ref), channel_id=1, source_target_pairs={{0,1},{1,0},{2,3},{3,2},{4,5},{5,4},{6,7},{7,6},{8,9},{9,8},{10,11... | collective-permute-start | bytes 786440 | tf_op jit(solution)/shard_map/ppermute | solution.py:581
  38.4 0.1 collective-permute-start.1
  38.5 0.8 shard_map.88
  39.3 0.4 collective-permute-done.1.taken_ref
  39.7 0.0 collective-permute-done.partner_ref
  39.7 12.9 %shard_map.89 = (f32[512,128]{1,0:T(8,128)S(1)}, f32[512,128]{1,0:T(8,128)S(1)}) custom-call(f32[512,128]{1,0:T(8,128)S(1)} %get-tuple-element.19.coeffs_ref, f32[512,128]{1,0:T(8,128)S(1)} %collective-permute-done.partner_ref, f32[32,32,128]{2,1,0:T(8,128)S(1)} %get-tuple-element.20.leaf_ref, f32[768,128]{1,0:T(8,128)S(1)} %get-tuple-element.21.points_ref, ...), custom_call_target="tpu_custom_call" | custom-call | flops 1000000 | bytes 1000000 | tf_op jit(solution)/shard_map/pallas_call | solution.py:585
  52.6 18.9 %all_to_all.15 = f32[512,1,128]{2,1,0:T(1,128)S(1)} all-to-all(f32[512,1,128]{2,1,0:T(1,128)S(1)} %bitcast.23), channel_id=1, replica_groups=mesh['box_0'=4,'box_1'=8,'box_2'=4,'box_3'=2] {'box_0','box_1','box_2'}, dimensions={0} | all-to-all | bytes 524288 | tf_op jit(solution)/shard_map/all_to_all | solution.py:523
  71.5 0.1 shard_map.90.mine_ref
  71.7 2.7 %collective-permute-start.2 = (f32[8,128]{1,0:T(8,128)S(1)}, f32[8,128]{1,0:T(8,128)S(1)}, u32[]{:S(2)}, u32[]{:S(2)}) collective-permute-start(f32[8,128]{1,0:T(8,128)S(1)} %shard_map.90.mine_ref), channel_id=1, source_target_pairs={{0,1},{1,0},{2,3},{3,2},{4,5},{5,4},{6,7},{7,6},{8,9},{9,8},{10,11... | collective-permute-start | bytes 12296 | tf_op jit(solution)/shard_map/ppermute | solution.py:600
  74.4 0.8 collective-permute-done.2.theirs_ref
  75.2 0.6 shard_map.91
  75.8 21.0 %all_to_all.16 = f32[768,1,128]{2,1,0:T(1,128)S(1)} all-to-all(f32[768,1,128]{2,1,0:T(1,128)S(1)} %bitcast.22), channel_id=1, replica_groups=mesh['box_0'=4,'box_1'=8,'box_2'=4,'box_3'=2] {'box_0','box_1','box_2'}, dimensions={0} | all-to-all | bytes 786432 | tf_op jit(solution)/shard_map/all_to_all | solution.py:523
  96.8 0.0 copy-done.1
  96.8 1.5 %shard_map.92 = (f32[16,4096]{1,0:T(8,128)}, f32[16,2048]{1,0:T(8,128)}) custom-call(f32[768,128]{1,0:T(8,128)S(1)} %bitcast.20, f32[2,128]{1,0:T(2,128)S(1)} %get-tuple-element.29.scalars_ref, f32[16,4096]{1,0:T(8,128)S(1)} %copy-done.1), custom_call_target="tpu_custom_call" | custom-call | flops 1000000 | bytes 1000000 | tf_op jit(solution)/shard_map/pallas_call | solution.py:604
  (4 shorter events, 0.0 us)
Async XLA Ops:
  3.1 31.3 %all-to-all-start = ((f32[768,1,128]{2,1,0:T(1,128)}), f32[768,1,128]{2,1,0:T(1,128)S(1)}, u32[]{:S(2)}, u32[]{:S(2)}) async-start(f32[768,1,128]{2,1,0:T(1,128)} %bitcast.28), calls=%async_computation | async-start | bytes 786432 | tf_op jit(solution)/shard_map/all_to_all | solution.py:523
  20.3 1.0 copy-start
  21.2 0.7 copy-start.2
  21.9 0.7 copy-start.3
  34.4 62.4 %copy-start.1 = (f32[16,4096]{1,0:T(8,128)S(1)}, f32[16,4096]{1,0:T(8,128)}, u32[]{:S(2)}) copy-start(f32[16,4096]{1,0:T(8,128)} %v_ref.1) | copy-start | bytes 786436
  35.3 4.4 %collective-permute-start = (f32[512,128]{1,0:T(8,128)S(1)}, f32[512,128]{1,0:T(8,128)S(1)}, u32[]{:S(2)}, u32[]{:S(2)}) collective-permute-start(f32[512,128]{1,0:T(8,128)S(1)} %get-tuple-element.19.coeffs_ref), channel_id=1, source_target_pairs={{0,1},{1,0},{2,3},{3,2},{4,5},{5,4},{6,7},{7,6},{8,9},{9,8},{10,11... | collective-permute-start | bytes 786440 | tf_op jit(solution)/shard_map/ppermute | solution.py:581
  38.4 1.3 %collective-permute-start.1 = (f32[128,128]{1,0:T(8,128)S(1)}, f32[128,128]{1,0:T(8,128)S(1)}, u32[]{:S(2)}, u32[]{:S(2)}) collective-permute-start(f32[128,128]{1,0:T(8,128)S(1)} %get-tuple-element.24), channel_id=1, source_target_pairs={{0,1},{1,0},{2,3},{3,2},{4,5},{5,4},{6,7},{7,6},{8,9},{9,8},{10,11... | collective-permute-start | bytes 196616 | tf_op jit(solution)/shard_map/ppermute | solution.py:575
  71.7 3.5 %collective-permute-start.2 = (f32[8,128]{1,0:T(8,128)S(1)}, f32[8,128]{1,0:T(8,128)S(1)}, u32[]{:S(2)}, u32[]{:S(2)}) collective-permute-start(f32[8,128]{1,0:T(8,128)S(1)} %shard_map.90.mine_ref), channel_id=1, source_target_pairs={{0,1},{1,0},{2,3},{3,2},{4,5},{5,4},{6,7},{7,6},{8,9},{9,8},{10,11... | collective-permute-start | bytes 12296 | tf_op jit(solution)/shard_map/ppermute | solution.py:600

commit v5 on v4

--- a/solution.py
+++ b/solution.py
@@ -244,14 +244,10 @@
         copy.start()
 
     def leave(k):
-        return pltpu.make_async_copy(maps.at[k & 1], maps_hbm.at[k - 1], map_sems.at[k & 1])
+        return pltpu.make_async_copy(maps.at[k - 1], maps_hbm.at[k - 1], map_sems.at[k - 1])
 
     def section(k, carry):
-        @pl.when(k > 2)
-        def _():
-            leave(k - 2).wait()
-
-        section_maps(info_ref, k, maps.at[k & 1])
+        section_maps(info_ref, k, maps.at[k - 1])
         leave(k).start()
         return carry
 
@@ -269,7 +265,7 @@
     first = jnp.broadcast_to(first, (128, 128))
     keep_ref[...] = jnp.where(first, low, high)
     give_ref[...] = jnp.where(first, high, low)
-    for k in (SECTIONS - 2, SECTIONS - 1):
+    for k in range(1, SECTIONS):
         leave(k).wait()
 
 
@@ -551,7 +547,6 @@
         ],
         mib=60,
     )(basis_vector, coords, diagonal.reshape(32, 128), sketch_rows, sketch_signs)
-    map_pair = pltpu.VMEM((2, 2, WIDTH, WIDTH, 128), F32)
     tile = f32(CHIPS, 128)
     maps, keep, give = call(
         early_kernel,
@@ -561,11 +556,11 @@
             vector,
             ints,
             ints,
-            map_pair,
+            pltpu.VMEM((SECTIONS - 1, 2, WIDTH, WIDTH, 128), F32),
             parts,
             parts,
             pltpu.SemaphoreType.DMA((3,)),
-            pltpu.SemaphoreType.DMA((2,)),
+            pltpu.SemaphoreType.DMA((SECTIONS - 1,)),
         ],
         outs=(HBM, VMEM, VMEM),
         flops=20000000,

time: 98.8 us -> 98.8 us (level)
  waiting for transfers between devices: 7.04 us -> 9.15 us
  Pallas kernels: 25.2 us -> 23.1 us
    all_to_all x1, waiting for transfers between devices: 5.84 us -> 7.95 us  [exchange(): return lax.all_to_all(x[:, None, :], CHIP, 0, 0, tiled=True)[:, 0, :]]
    pallas_call x1, Pallas kernels: 5.92 us -> 3.82 us  [body(): call(early_kernel, (f32(SECTIONS - 1, 2, WIDTH, WIDTH, 128), tile, tile),...]
  transfers between devices with their start and end apart: 4 -> 4, of which waited for: 3 -> 3; matrix products, arithmetic and copies ran while one was open for 0% -> 0% of each run, Pallas kernels for 7% -> 5%
where the time goes in v5:
time: 98.8 us; the launch traced here: 98.3 us
  blocking collectives  40 us (40%)
  Pallas kernels  23.1 us (23%)
  starting transfers between devices  22.3 us (23%)
  waiting for transfers between devices  9.15 us (9%)
  local copies, waits for them, and re-layouts  2.55 us (3%)
  between operations  1.37 us (1%)
    all_to_all x2, blocking collectives, exchange(): return lax.all_to_all(x[:, None, :], CHIP, 0, 0, tiled=True)[:, 0, :]  40 us
    all_to_all x1, starting transfers between devices, exchange(): return lax.all_to_all(x[:, None, :], CHIP, 0, 0, tiled=True)[:, 0, :]  16.3 us
    pallas_call x1, Pallas kernels, body(): call(core_kernel, (f32(CHIPS * SUM_ROWS, 128), f32(512, 128)), [VMEM] * 8...  12.9 us
    all_to_all x1, waiting for transfers between devices, exchange(): return lax.all_to_all(x[:, None, :], CHIP, 0, 0, tiled=True)[:, 0, :]  7.95 us
    pallas_call x1, Pallas kernels, body(): call(early_kernel, (f32(SECTIONS - 1, 2, WIDTH, WIDTH, 128), tile, tile),...  3.82 us
    ppermute x1, starting transfers between devices, body(): partner = lax.ppermute(coeffs, CORE, swap)  3.1 us
    ppermute x1, starting transfers between devices, body(): theirs = lax.ppermute(mine, CORE, swap)  2.72 us
    pallas_call x1, Pallas kernels, body(): call(pack_kernel, f32(CHIPS * OUT_ROWS, 128), [HBM] * 5, [vector, pltpu.V...  2.46 us
  transfers between devices with their start and end apart: 4, of which 3 were waited for; matrix products, arithmetic and copies ran while one was open for 0% of the time, Pallas kernels for 5%

profile of v5, /device:TPU:1, one launch (start us, length us, event | category | flops | bytes accessed | tf_op | source)
XLA Modules:
  0.0 98.3 jit_solution(9588754968273936787)
XLA Ops:
  0.6 2.5 %shard_map.85 = f32[768,128]{1,0:T(8,128)} custom-call(f32[16,4096]{1,0:T(8,128)} %v_ref.1, s32[2,4096]{1,0:T(2,128)} %refs_1_.1, f32[32,128]{1,0:T(8,128)} %bitcast.29, s32[32,128]{1,0:T(8,128)} %bitcast.24, s32[32,128]{1,0:T(8,128)} %bitcast.26), custom_call_target="tpu_custom_call" | custom-call | flops 1000000 | bytes 1000000 | tf_op jit(solution)/shard_map/pallas_call | solution.py:535
  3.1 16.3 %all-to-all-start = ((f32[768,1,128]{2,1,0:T(1,128)}), f32[768,1,128]{2,1,0:T(1,128)S(1)}, u32[]{:S(2)}, u32[]{:S(2)}) async-start(f32[768,1,128]{2,1,0:T(1,128)} %bitcast.28), calls=%async_computation | async-start | bytes 786432 | tf_op jit(solution)/shard_map/all_to_all | solution.py:519
  20.1 0.1 stack.20
  20.2 0.1 broadcast_in_dim.15.info_ref
  20.3 1.0 copy-done
  21.2 0.7 copy-done.2
  21.9 0.7 copy-done.3
  22.7 3.8 %shard_map.86 = (f32[7,2,32,32,128]{4,3,2,1,0:T(8,128)}, f32[128,128]{1,0:T(8,128)S(1)}, f32[128,128]{1,0:T(8,128)S(1)}) custom-call(s32[8,128]{1,0:T(8,128)S(1)} %broadcast_in_dim.15.info_ref, f32[16,4096]{1,0:T(8,128)S(1)} %copy-done, s32[32,128]{1,0:T(8,128)S(1)} %bitcast.25, s32[32,128]{1,0:T(8,128)S(1)} %bitcast.27), custom_call_target="tpu_custom_call" | custom-call | flops 20000000 | bytes 1000000 | tf_op jit(solution)/shard_map/pallas_call | solution.py:551
  26.5 7.9 %all-to-all-done = f32[768,1,128]{2,1,0:T(1,128)S(1)} async-done(((f32[768,1,128]{2,1,0:T(1,128)}), f32[768,1,128]{2,1,0:T(1,128)S(1)}, u32[]{:S(2)}, u32[]{:S(2)}) %all-to-all-start) | async-done | bytes 393248 | tf_op jit(solution)/shard_map/all_to_all | solution.py:519
  34.4 0.9 shard_map.87
  35.3 3.1 %collective-permute-start = (f32[512,128]{1,0:T(8,128)S(1)}, f32[512,128]{1,0:T(8,128)S(1)}, u32[]{:S(2)}, u32[]{:S(2)}) collective-permute-start(f32[512,128]{1,0:T(8,128)S(1)} %get-tuple-element.19.coeffs_ref), channel_id=1, source_target_pairs={{0,1},{1,0},{2,3},{3,2},{4,5},{5,4},{6,7},{7,6},{8,9},{9,8},{10,11... | collective-permute-start | bytes 786440 | tf_op jit(solution)/shard_map/ppermute | solution.py:576
  38.4 0.1 collective-permute-start.1
  38.5 0.8 shard_map.88
  39.3 0.4 collective-permute-done.1.taken_ref
  39.7 0.0 collective-permute-done.partner_ref
  39.7 12.9 %shard_map.89 = (f32[512,128]{1,0:T(8,128)S(1)}, f32[512,128]{1,0:T(8,128)S(1)}) custom-call(f32[512,128]{1,0:T(8,128)S(1)} %get-tuple-element.19.coeffs_ref, f32[512,128]{1,0:T(8,128)S(1)} %collective-permute-done.partner_ref, f32[32,32,128]{2,1,0:T(8,128)S(1)} %get-tuple-element.20.leaf_ref, f32[768,128]{1,0:T(8,128)S(1)} %get-tuple-element.21.points_ref, ...), custom_call_target="tpu_custom_call" | custom-call | flops 1000000 | bytes 1000000 | tf_op jit(solution)/shard_map/pallas_call | solution.py:580
  52.6 18.9 %all_to_all.15 = f32[512,1,128]{2,1,0:T(1,128)S(1)} all-to-all(f32[512,1,128]{2,1,0:T(1,128)S(1)} %bitcast.23), channel_id=1, replica_groups=mesh['box_0'=4,'box_1'=8,'box_2'=4,'box_3'=2] {'box_0','box_1','box_2'}, dimensions={0} | all-to-all | bytes 524288 | tf_op jit(solution)/shard_map/all_to_all | solution.py:519
  71.5 0.1 shard_map.90.mine_ref
  71.7 2.7 %collective-permute-start.2 = (f32[8,128]{1,0:T(8,128)S(1)}, f32[8,128]{1,0:T(8,128)S(1)}, u32[]{:S(2)}, u32[]{:S(2)}) collective-permute-start(f32[8,128]{1,0:T(8,128)S(1)} %shard_map.90.mine_ref), channel_id=1, source_target_pairs={{0,1},{1,0},{2,3},{3,2},{4,5},{5,4},{6,7},{7,6},{8,9},{9,8},{10,11... | collective-permute-start | bytes 12296 | tf_op jit(solution)/shard_map/ppermute | solution.py:595
  74.4 0.8 collective-permute-done.2.theirs_ref
  75.2 0.6 shard_map.91
  75.8 21.0 %all_to_all.16 = f32[768,1,128]{2,1,0:T(1,128)S(1)} all-to-all(f32[768,1,128]{2,1,0:T(1,128)S(1)} %bitcast.22), channel_id=1, replica_groups=mesh['box_0'=4,'box_1'=8,'box_2'=4,'box_3'=2] {'box_0','box_1','box_2'}, dimensions={0} | all-to-all | bytes 786432 | tf_op jit(solution)/shard_map/all_to_all | solution.py:519
  96.8 0.0 copy-done.1
  96.8 1.5 %shard_map.92 = (f32[16,4096]{1,0:T(8,128)}, f32[16,2048]{1,0:T(8,128)}) custom-call(f32[768,128]{1,0:T(8,128)S(1)} %bitcast.20, f32[2,128]{1,0:T(2,128)S(1)} %get-tuple-element.29.scalars_ref, f32[16,4096]{1,0:T(8,128)S(1)} %copy-done.1), custom_call_target="tpu_custom_call" | custom-call | flops 1000000 | bytes 1000000 | tf_op jit(solution)/shard_map/pallas_call | solution.py:599
  (4 shorter events, 0.0 us)
Async XLA Ops:
  3.1 31.3 %all-to-all-start = ((f32[768,1,128]{2,1,0:T(1,128)}), f32[768,1,128]{2,1,0:T(1,128)S(1)}, u32[]{:S(2)}, u32[]{:S(2)}) async-start(f32[768,1,128]{2,1,0:T(1,128)} %bitcast.28), calls=%async_computation | async-start | bytes 786432 | tf_op jit(solution)/shard_map/all_to_all | solution.py:519
  20.3 1.0 copy-start
  21.2 0.7 copy-start.2
  21.9 0.7 copy-start.3
  34.4 62.4 %copy-start.1 = (f32[16,4096]{1,0:T(8,128)S(1)}, f32[16,4096]{1,0:T(8,128)}, u32[]{:S(2)}) copy-start(f32[16,4096]{1,0:T(8,128)} %v_ref.1) | copy-start | bytes 786436
  35.3 4.4 %collective-permute-start = (f32[512,128]{1,0:T(8,128)S(1)}, f32[512,128]{1,0:T(8,128)S(1)}, u32[]{:S(2)}, u32[]{:S(2)}) collective-permute-start(f32[512,128]{1,0:T(8,128)S(1)} %get-tuple-element.19.coeffs_ref), channel_id=1, source_target_pairs={{0,1},{1,0},{2,3},{3,2},{4,5},{5,4},{6,7},{7,6},{8,9},{9,8},{10,11... | collective-permute-start | bytes 786440 | tf_op jit(solution)/shard_map/ppermute | solution.py:576
  38.4 1.3 %collective-permute-start.1 = (f32[128,128]{1,0:T(8,128)S(1)}, f32[128,128]{1,0:T(8,128)S(1)}, u32[]{:S(2)}, u32[]{:S(2)}) collective-permute-start(f32[128,128]{1,0:T(8,128)S(1)} %get-tuple-element.24), channel_id=1, source_target_pairs={{0,1},{1,0},{2,3},{3,2},{4,5},{5,4},{6,7},{7,6},{8,9},{9,8},{10,11... | collective-permute-start | bytes 196616 | tf_op jit(solution)/shard_map/ppermute | solution.py:570
  71.7 3.5 %collective-permute-start.2 = (f32[8,128]{1,0:T(8,128)S(1)}, f32[8,128]{1,0:T(8,128)S(1)}, u32[]{:S(2)}, u32[]{:S(2)}) collective-permute-start(f32[8,128]{1,0:T(8,128)S(1)} %shard_map.90.mine_ref), channel_id=1, source_target_pairs={{0,1},{1,0},{2,3},{3,2},{4,5},{5,4},{6,7},{7,6},{8,9},{9,8},{10,11... | collective-permute-start | bytes 12296 | tf_op jit(solution)/shard_map/ppermute | solution.py:595

commit v6 on v5

--- a/solution.py
+++ b/solution.py
@@ -269,15 +269,25 @@
         leave(k).wait()
 
 
-def hot_kernel(info_ref, points_ref, rhs_ref, maps_ref):
+def hot_kernel(info_ref, points_ref, coeffs_ref, rhs_ref, maps_ref, begun_ref):
     for s in range(LEAF):
         low = points_ref[pl.ds(512 + s * 8 + 3, 1), :].astype(jnp.int32) & 255
         hot_rows(rhs_ref, low, pl.ds(s * 128, 128))
     section_maps(info_ref, 0, maps_ref)
 
+    def store(a, x):
+        begun_ref[row16(a), :] = jnp.concatenate(x, 0)
+
+    product(
+        WIDTH,
+        [(lambda a, b: maps_ref[0, a, pl.ds(b, 1), :], lambda b: halves(coeffs_ref, b))],
+        store,
+        lambda a: [0.85 * x for x in halves(coeffs_ref, a)],
+    )
+
 
 def core_kernel(
-    coeffs_ref,
+    begun_ref,
     partner_ref,
     leaf_ref,
     points_ref,
@@ -304,10 +314,8 @@
 
     copy(jnp.int32(1)).start()
     copy(jnp.int32(2)).start()
-    now[0] = coeffs_ref[...]
-    other[0] = partner_ref[...]
-
-    def section(k, own, cross):
+
+    def section(k, terms, start):
         at = k & 1
         step = jnp.left_shift(1, jnp.minimum(k, SECTIONS - 2))
         across = lanes ^ step
@@ -318,27 +326,33 @@
                 [jnp.take_along_axis(y, across, axis=1, mode="promise_in_bounds") for y in x], 0
             )
 
-        product(
-            WIDTH,
-            [
+        product(WIDTH, terms(at), store, start)
+
+    section(
+        jnp.int32(0),
+        lambda at: [
+            (lambda a, b: first[1, a, pl.ds(b, 1), :], lambda b: halves(partner_ref, b)),
+        ],
+        lambda a: halves(begun_ref, a),
+    )
+
+    def later(k, carry):
+        copy(k).wait()
+
+        @pl.when(k < SECTIONS - 2)
+        def _():
+            copy(k + 2).start()
+
+        slot = lax.rem(k, 3)
+        own, cross = maps.at[slot, 0], maps.at[slot, 1]
+        section(
+            k,
+            lambda at: [
                 (lambda a, b: own[a, pl.ds(b, 1), :], lambda b: halves(now, b, at)),
                 (lambda a, b: cross[a, pl.ds(b, 1), :], lambda b: halves(other, b, at)),
             ],
-            store,
-            lambda a: [0.85 * x for x in jnp.split(now[at, row16(a), :], 2)],
+            lambda a: [0.85 * x for x in halves(now, a, k & 1)],
         )
-
-    section(jnp.int32(0), first.at[0], first.at[1])
-
-    def later(k, carry):
-        copy(k).wait()
-
-        @pl.when(k < SECTIONS - 2)
-        def _():
-            copy(k + 2).start()
-
-        slot = lax.rem(k, 3)
-        section(k, maps.at[slot, 0], maps.at[slot, 1])
         return carry
 
     lax.fori_loop(1, SECTIONS, later, 0)
@@ -377,7 +391,7 @@
         energy += r * r
         mixed += r * v
     for c in range(4):
-        image_ref[pl.ds(c * 128, 128), :] = image[pl.ds(c * 128, 128), :].T
+        image_ref[pl.ds(c, 128, stride=BACK_ROWS), :] = image[pl.ds(c * 128, 128), :].T
     for half, tile in enumerate(sketched(lhs, rhs)):
         out_ref[pl.ds(half, 128, stride=SUM_ROWS), :] = tile
     out_ref[pl.ds(2, 128, stride=SUM_ROWS), :] = keep_ref[...] + taken_ref[...]
@@ -425,8 +439,6 @@
 
 
 def chunk_kernel(mine_ref, theirs_ref, image_ref, out_ref, arnoldi_ref, scalars_ref):
-    for c in range(4):
-        out_ref[pl.ds(c, 128, stride=BACK_ROWS), :] = image_ref[pl.ds(c * 128, 128), :]
     both = [(mine_ref[4 + i : 5 + i, :], theirs_ref[4 + i : 5 + i, :]) for i in range(4)]
     vv, p, e, cr = both
     square = vv[0] + vv[1]
@@ -502,7 +514,7 @@
     return jax.ShapeDtypeStruct(shape, F32)
 
 
-def call(kernel, out, ins, scratch=(), flops=1000000, mib=12, outs=None):
+def call(kernel, out, ins, scratch=(), flops=1000000, mib=12, outs=None, alias=None):
     single = not isinstance(out, tuple)
     return pl.pallas_call(
         kernel,
@@ -510,6 +522,7 @@
         in_specs=ins,
         out_specs=outs or (VMEM if single else tuple(VMEM for _ in out)),
         scratch_shapes=list(scratch),
+        input_output_aliases=alias or {},
         cost_estimate=pl.CostEstimate(flops=flops, bytes_accessed=1000000, transcendentals=0),
         compiler_params=pltpu.CompilerParams(vmem_limit_bytes=mib * 1024 * 1024),
     )
@@ -572,14 +585,16 @@
         leaf_kernel,
         (f32(512, 128), f32(WIDTH, LEAF, 128), f32(OUT_ROWS * 128, 128)),
         [VMEM, VMEM, HBM],
-    )(info, got, keep)
+    )(info, got, taken)
     partner = lax.ppermute(coeffs, CORE, swap)
     first_type = f32(2, WIDTH, WIDTH, 128)
-    hot, first = call(hot_kernel, (hot_type, first_type), [VMEM, VMEM])(info, held)
+    hot, first, begun = call(
+        hot_kernel, (hot_type, first_type, f32(512, 128)), [VMEM] * 3
+    )(info, held, coeffs)
     pair = pltpu.VMEM((2, 512, 128), F32)
     parts_out, image = call(
         core_kernel,
-        (f32(CHIPS * SUM_ROWS, 128), f32(512, 128)),
+        (f32(CHIPS * SUM_ROWS, 128), f32(CHIPS * BACK_ROWS, 128)),
         [VMEM] * 8 + [HBM],
         [
             pair,
@@ -590,11 +605,14 @@
             pltpu.SemaphoreType.DMA((3,)),
         ],
         mib=CORE_MIB,
-    )(coeffs, partner, leaf, held, first, hot, keep, taken, maps)
+    )(begun, partner, leaf, held, first, hot, keep, taken, maps)
     mine = call(sum_kernel, f32(8, 128), [VMEM, VMEM])(info, exchange(parts_out))
     theirs = lax.ppermute(mine, CORE, swap)
     back, arnoldi, scalars = call(
-        chunk_kernel, (f32(CHIPS * BACK_ROWS, 128), f32(2, NRHS), f32(2, 128)), [VMEM] * 3
+        chunk_kernel,
+        (f32(CHIPS * BACK_ROWS, 128), f32(2, NRHS), f32(2, 128)),
+        [VMEM] * 3,
+        alias={2: 0},
     )(mine, theirs, image)
     new_basis, sketch = call(
         last_kernel,

time: 98.8 us -> 98.8 us (level)
  waiting for transfers between devices: 9.15 us -> 7.73 us
    all_to_all x1, waiting for transfers between devices: 7.95 us -> 6 us  [exchange(): return lax.all_to_all(x[:, None, :], CHIP, 0, 0, tiled=True)[:, 0, :]]
where the time goes in v6:
time: 98.8 us; the launch traced here: 98.3 us
  blocking collectives  40.3 us (41%)
  Pallas kernels  23.5 us (24%)
  starting transfers between devices  22.9 us (23%)
  waiting for transfers between devices  7.73 us (8%)
  local copies, waits for them, and re-layouts  2.55 us (3%)
  between operations  1.37 us (1%)
    all_to_all x2, blocking collectives, exchange(): return lax.all_to_all(x[:, None, :], CHIP, 0, 0, tiled=True)[:, 0, :]  40.3 us
    all_to_all x1, starting transfers between devices, exchange(): return lax.all_to_all(x[:, None, :], CHIP, 0, 0, tiled=True)[:, 0, :]  16.3 us
    pallas_call x1, Pallas kernels, body(): call(core_kernel, (f32(CHIPS * SUM_ROWS, 128), f32(CHIPS * BACK_ROWS, 128...  12.7 us
    all_to_all x1, waiting for transfers between devices, exchange(): return lax.all_to_all(x[:, None, :], CHIP, 0, 0, tiled=True)[:, 0, :]  6 us
    pallas_call x1, Pallas kernels, body(): call(early_kernel, (f32(SECTIONS - 1, 2, WIDTH, WIDTH, 128), tile, tile),...  3.82 us
    ppermute x1, starting transfers between devices, body(): partner = lax.ppermute(coeffs, CORE, swap)  3.1 us
    pallas_call x1, Pallas kernels, body(): call(pack_kernel, f32(CHIPS * OUT_ROWS, 128), [HBM] * 5, [vector, pltpu.V...  2.46 us
    ppermute x1, starting transfers between devices, body(): theirs = lax.ppermute(mine, CORE, swap)  2.39 us
  transfers between devices with their start and end apart: 4, of which 3 were waited for; matrix products, arithmetic and copies ran while one was open for 0% of the time, Pallas kernels for 5%

profile of v6, /device:TPU:1, one launch (start us, length us, event | category | flops | bytes accessed | tf_op | source)
XLA Modules:
  0.0 98.3 jit_solution(12634828637737768519)
XLA Ops:
  0.6 2.5 %shard_map.85 = f32[768,128]{1,0:T(8,128)} custom-call(f32[16,4096]{1,0:T(8,128)} %v_ref.1, s32[2,4096]{1,0:T(2,128)} %refs_1_.1, f32[32,128]{1,0:T(8,128)} %bitcast.29, s32[32,128]{1,0:T(8,128)} %bitcast.24, s32[32,128]{1,0:T(8,128)} %bitcast.26), custom_call_target="tpu_custom_call" | custom-call | flops 1000000 | bytes 1000000 | tf_op jit(solution)/shard_map/pallas_call | solution.py:548
  3.1 16.3 %all-to-all-start = ((f32[768,1,128]{2,1,0:T(1,128)}), f32[768,1,128]{2,1,0:T(1,128)S(1)}, u32[]{:S(2)}, u32[]{:S(2)}) async-start(f32[768,1,128]{2,1,0:T(1,128)} %bitcast.28), calls=%async_computation | async-start | bytes 786432 | tf_op jit(solution)/shard_map/all_to_all | solution.py:532
  20.1 0.1 stack.20
  20.2 0.1 broadcast_in_dim.15.info_ref
  20.3 1.0 copy-done
  21.2 0.7 copy-done.2
  21.9 0.7 copy-done.3
  22.7 3.8 %shard_map.86 = (f32[7,2,32,32,128]{4,3,2,1,0:T(8,128)}, f32[128,128]{1,0:T(8,128)S(1)}, f32[128,128]{1,0:T(8,128)S(1)}) custom-call(s32[8,128]{1,0:T(8,128)S(1)} %broadcast_in_dim.15.info_ref, f32[16,4096]{1,0:T(8,128)S(1)} %copy-done, s32[32,128]{1,0:T(8,128)S(1)} %bitcast.25, s32[32,128]{1,0:T(8,128)S(1)} %bitcast.27), custom_call_target="tpu_custom_call" | custom-call | flops 20000000 | bytes 1000000 | tf_op jit(solution)/shard_map/pallas_call | solution.py:564
  26.5 1.0 %collective-permute-start = (f32[128,128]{1,0:T(8,128)S(1)}, f32[128,128]{1,0:T(8,128)S(1)}, u32[]{:S(2)}, u32[]{:S(2)}) collective-permute-start(f32[128,128]{1,0:T(8,128)S(1)} %get-tuple-element.19), channel_id=1, source_target_pairs={{0,1},{1,0},{2,3},{3,2},{4,5},{5,4},{6,7},{7,6},{8,9},{9,8},{10,11... | collective-permute-start | bytes 196616 | tf_op jit(solution)/shard_map/ppermute | solution.py:583
  27.5 0.9 collective-permute-done.after_ref.taken_ref
  28.4 6.0 %all-to-all-done = f32[768,1,128]{2,1,0:T(1,128)S(1)} async-done(((f32[768,1,128]{2,1,0:T(1,128)}), f32[768,1,128]{2,1,0:T(1,128)S(1)}, u32[]{:S(2)}, u32[]{:S(2)}) %all-to-all-start) | async-done | bytes 393248 | tf_op jit(solution)/shard_map/all_to_all | solution.py:532
  34.4 0.9 shard_map.87
  35.3 3.1 %collective-permute-start.1 = (f32[512,128]{1,0:T(8,128)S(1)}, f32[512,128]{1,0:T(8,128)S(1)}, u32[]{:S(2)}, u32[]{:S(2)}) collective-permute-start(f32[512,128]{1,0:T(8,128)S(1)} %get-tuple-element.21.coeffs_ref), channel_id=1, source_target_pairs={{0,1},{1,0},{2,3},{3,2},{4,5},{5,4},{6,7},{7,6},{8,9},{9,8},{10,11... | collective-permute-start | bytes 786440 | tf_op jit(solution)/shard_map/ppermute | solution.py:589
  38.4 1.4 %shard_map.88 = (bf16[256,4096]{1,0:T(8,128)(2,1)S(1)}, f32[2,32,32,128]{3,2,1,0:T(8,128)S(1)}, f32[512,128]{1,0:T(8,128)S(1)}) custom-call(s32[8,128]{1,0:T(8,128)S(1)} %broadcast_in_dim.15.info_ref, f32[768,128]{1,0:T(8,128)S(1)} %get-tuple-element.20.points_ref, f32[512,128]{1,0:T(8,128)S(1)} %get-tuple-element.21.coeffs_ref), custom_call_target="tpu_custom_call" | custom-call | flops 1000000 | bytes 1000000 | tf_op jit(solution)/shard_map/pallas_call | solution.py:591
  39.8 0.0 collective-permute-done.1.partner_ref
  39.8 12.7 %shard_map.89 = (f32[512,128]{1,0:T(8,128)S(1)}, f32[768,128]{1,0:T(8,128)S(1)}) custom-call(f32[512,128]{1,0:T(8,128)S(1)} %get-tuple-element.22.begun_ref, f32[512,128]{1,0:T(8,128)S(1)} %collective-permute-done.1.partner_ref, f32[32,32,128]{2,1,0:T(8,128)S(1)} %get-tuple-element.23.leaf_ref, f32[768,128]{1,0:T(8,128)S(1)} %get-tuple-element.20.points_ref, ...), custom_call_target="tpu_custom_call" | custom-call | flops 1000000 | bytes 1000000 | tf_op jit(solution)/shard_map/pallas_call | solution.py:595
  52.6 19.3 %all_to_all.15 = f32[512,1,128]{2,1,0:T(1,128)S(1)} all-to-all(f32[512,1,128]{2,1,0:T(1,128)S(1)} %bitcast.23), channel_id=1, replica_groups=mesh['box_0'=4,'box_1'=8,'box_2'=4,'box_3'=2] {'box_0','box_1','box_2'}, dimensions={0} | all-to-all | bytes 524288 | tf_op jit(solution)/shard_map/all_to_all | solution.py:532
  71.8 0.1 shard_map.90.mine_ref
  72.0 2.4 %collective-permute-start.2 = (f32[8,128]{1,0:T(8,128)S(1)}, f32[8,128]{1,0:T(8,128)S(1)}, u32[]{:S(2)}, u32[]{:S(2)}) collective-permute-start(f32[8,128]{1,0:T(8,128)S(1)} %shard_map.90.mine_ref), channel_id=1, source_target_pairs={{0,1},{1,0},{2,3},{3,2},{4,5},{5,4},{6,7},{7,6},{8,9},{9,8},{10,11... | collective-permute-start | bytes 12296 | tf_op jit(solution)/shard_map/ppermute | solution.py:610
  74.4 0.8 collective-permute-done.2.theirs_ref
  75.2 0.6 shard_map.91
  75.8 21.0 %all_to_all.16 = f32[768,1,128]{2,1,0:T(1,128)S(1)} all-to-all(f32[768,1,128]{2,1,0:T(1,128)S(1)} %bitcast.20), channel_id=1, replica_groups=mesh['box_0'=4,'box_1'=8,'box_2'=4,'box_3'=2] {'box_0','box_1','box_2'}, dimensions={0} | all-to-all | bytes 786432 | tf_op jit(solution)/shard_map/all_to_all | solution.py:532
  96.8 0.0 copy-done.1
  96.8 1.5 %shard_map.92 = (f32[16,4096]{1,0:T(8,128)}, f32[16,2048]{1,0:T(8,128)}) custom-call(f32[768,128]{1,0:T(8,128)S(1)} %bitcast.21, f32[2,128]{1,0:T(2,128)S(1)} %get-tuple-element.31.scalars_ref, f32[16,4096]{1,0:T(8,128)S(1)} %copy-done.1), custom_call_target="tpu_custom_call" | custom-call | flops 1000000 | bytes 1000000 | tf_op jit(solution)/shard_map/pallas_call | solution.py:617
  (4 shorter events, 0.0 us)
Async XLA Ops:
  3.1 31.3 %all-to-all-start = ((f32[768,1,128]{2,1,0:T(1,128)}), f32[768,1,128]{2,1,0:T(1,128)S(1)}, u32[]{:S(2)}, u32[]{:S(2)}) async-start(f32[768,1,128]{2,1,0:T(1,128)} %bitcast.28), calls=%async_computation | async-start | bytes 786432 | tf_op jit(solution)/shard_map/all_to_all | solution.py:532
  20.3 1.0 copy-start
  21.2 0.7 copy-start.2
  21.9 0.7 copy-start.3
  26.5 1.9 %collective-permute-start = (f32[128,128]{1,0:T(8,128)S(1)}, f32[128,128]{1,0:T(8,128)S(1)}, u32[]{:S(2)}, u32[]{:S(2)}) collective-permute-start(f32[128,128]{1,0:T(8,128)S(1)} %get-tuple-element.19), channel_id=1, source_target_pairs={{0,1},{1,0},{2,3},{3,2},{4,5},{5,4},{6,7},{7,6},{8,9},{9,8},{10,11... | collective-permute-start | bytes 196616 | tf_op jit(solution)/shard_map/ppermute | solution.py:583
  35.3 4.5 %collective-permute-start.1 = (f32[512,128]{1,0:T(8,128)S(1)}, f32[512,128]{1,0:T(8,128)S(1)}, u32[]{:S(2)}, u32[]{:S(2)}) collective-permute-start(f32[512,128]{1,0:T(8,128)S(1)} %get-tuple-element.21.coeffs_ref), channel_id=1, source_target_pairs={{0,1},{1,0},{2,3},{3,2},{4,5},{5,4},{6,7},{7,6},{8,9},{9,8},{10,11... | collective-permute-start | bytes 786440 | tf_op jit(solution)/shard_map/ppermute | solution.py:589
  38.4 58.4 %copy-start.1 = (f32[16,4096]{1,0:T(8,128)S(1)}, f32[16,4096]{1,0:T(8,128)}, u32[]{:S(2)}) copy-start(f32[16,4096]{1,0:T(8,128)} %v_ref.1) | copy-start | bytes 786436
  72.0 3.2 %collective-permute-start.2 = (f32[8,128]{1,0:T(8,128)S(1)}, f32[8,128]{1,0:T(8,128)S(1)}, u32[]{:S(2)}, u32[]{:S(2)}) collective-permute-start(f32[8,128]{1,0:T(8,128)S(1)} %shard_map.90.mine_ref), channel_id=1, source_target_pairs={{0,1},{1,0},{2,3},{3,2},{4,5},{5,4},{6,7},{7,6},{8,9},{9,8},{10,11... | collective-permute-start | bytes 12296 | tf_op jit(solution)/shard_map/ppermute | solution.py:610
